TPU v7x, 32 devices: a whole 2x2x4 slice. The times are simulated.
32 devices in a mesh: fsdp: 4 (over y, x), tensor: 8 (over z, core).
Axes of the slice: x: 2, y: 2, z: 4, core: 2. Of those that a mesh axis runs over, the one named last changes fastest.
Arguments:
- block_input: bfloat16 [8, 1536, 1152], P('fsdp', 'tensor'), may hold values from -6 to 6
- segment_ids: int32 [8, 1536], P('fsdp'), may hold values from -1 to 15, as said below
- norm_gains: float32 [2, 1152], replicated, may hold values from 0.5 to 1.5
- row_biases: float32 [4, 1152], replicated, may hold values from -0.15 to 0.15
- in_projection: bfloat16 [3, 1152, 1152], P(None, 'fsdp', 'tensor'), may hold values from -0.1875 to 0.1875
- query_value_bias: float32 [2, 1152], P(None, 'tensor'), may hold values from -0.12 to 0.12
- out_projection: bfloat16 [1152, 1152], P('tensor', 'fsdp'), may hold values from -4 to 4
- up_weight: bfloat16 [1152, 4304], P('fsdp', 'tensor'), may hold values from -0.1875 to 0.1875
- unit_bias: bfloat16 [4304], P('tensor'), may hold values from -3 to 3
- down_weight: bfloat16 [4304, 1152], P('tensor', 'fsdp'), may hold values from -0.1875 to 0.1875
- cotangent: bfloat16 [8, 1536, 1152], P('fsdp', 'tensor'), may hold values from -6 to 6
Outputs:
- block_output: bfloat16 [8, 1536, 1152], P('fsdp', 'tensor')
- input_grad: float32 [8, 1536, 1152], P('fsdp', 'tensor')
- norm_gains_grad: float32 [2, 1152], replicated
- row_biases_grad: float32 [4, 1152], replicated
- in_projection_grad: float32 [3, 1152, 1152], P(None, 'fsdp', 'tensor')
- query_value_bias_grad: float32 [2, 1152], P(None, 'tensor')
- out_projection_grad: float32 [1152, 1152], P('tensor', 'fsdp')
- up_weight_grad: float32 [1152, 4304], P('fsdp', 'tensor')
- unit_bias_grad: float32 [4304], P('tensor')
- down_weight_grad: float32 [4304, 1152], P('tensor', 'fsdp')
Inputs may be any that keep to these rules, and one draw needn't show every extreme that they name: `segment_ids`: row block b holds 2 images in order; image j is a run of 729 consecutive rows with the id b * 2 + j, and every other row is padding with the id -1.
All inputs are finite; a program needn't handle non-finite values.
Results may differ from a plain program's by a relative error of at most 0.012.
Values may be sent and summed in bfloat16 or wider, within the bound.
A program may use at most 192 MiB of HBM per device.

v0:
```python
import functools
import math

import jax
import jax.numpy as jnp
from jax import lax
from jax.experimental import pallas as pl
from jax.experimental.pallas import tpu as pltpu
from jax.sharding import Mesh
from jax.sharding import PartitionSpec as P

DH = 72
IMG = 729
IMG_MB = 2
EPS = 1e-06
GELU_C = 0.7978845608028654
F32 = jnp.float32
BF16 = jnp.bfloat16
FSDP = ("fy", "fx")
SCALE = DH ** (-0.5)
LOG2E = math.log2(math.e)


def norm_forward(values, norm_gain, norm_shift):
    center = values - jnp.mean(values, axis=-1, keepdims=True)
    factor = lax.rsqrt(jnp.mean(center * center, axis=-1, keepdims=True) + EPS)
    scaled = center * factor
    return (scaled * norm_gain + norm_shift, scaled, factor)


def norm_backward(upstream, scaled, factor, norm_gain):
    inside = upstream * norm_gain
    return factor * (
        inside
        - jnp.mean(inside, axis=-1, keepdims=True)
        - scaled * jnp.mean(inside * scaled, axis=-1, keepdims=True)
    )


def gelu(pre_act):
    return (
        0.5
        * pre_act
        * (1.0 + jnp.tanh(GELU_C * (pre_act + 0.044715 * pre_act * pre_act * pre_act)))
    )


def gelu_both(pre_act):
    square = pre_act * pre_act
    curve = jnp.tanh(GELU_C * pre_act * (1.0 + 0.044715 * square))
    rise = 0.5 * (1.0 + curve)
    slope = rise + 0.5 * pre_act * (1.0 - curve * curve) * GELU_C * (1.0 + 3.0 * 0.044715 * square)
    return pre_act * rise, slope


def gelu_back(pre_act, upstream):
    return jax.vjp(gelu, pre_act)[1](upstream)[0]


def dot_nn(left, right):
    return lax.dot_general(left, right, (((1,), (0,)), ((), ())), preferred_element_type=F32)


def dot_nt(left, right):
    return lax.dot_general(left, right, (((1,), (1,)), ((), ())), preferred_element_type=F32)


def dot_tn(left, right):
    return lax.dot_general(left, right, (((0,), (0,)), ((), ())), preferred_element_type=F32)


def sum_products(lefts, rights):
    total = dot_nt(lefts[0], rights[0])
    for left, right in zip(lefts[1:], rights[1:]):
        total = total + dot_nt(left, right)
    return total


def round_up(value, unit):
    return -(-value // unit) * unit


def swap(value, axis):
    return lax.ppermute(value, axis, [(0, 1), (1, 0)])


def slot_swap(value, stride, slots):
    return lax.ppermute(value, "slot", [(s, s ^ stride) for s in range(slots)])


def part_sum(value, parts):
    value = value.astype(BF16)
    if parts == 2:
        return value.astype(F32) + swap(value, "part").astype(F32)
    return lax.psum(value.astype(F32), "part")


def part_gather(value, parts):
    if parts == 2:
        other = swap(value, "part")
        first = lax.axis_index("part") == 0
        return jnp.stack([jnp.where(first, value, other), jnp.where(first, other, value)])
    return lax.all_gather(value, "part", axis=0)


def add_half(left, right):
    return (left.astype(F32) + right.astype(F32)).astype(BF16)


MESH = pl.DeviceIdType.MESH


class Place:
    def __init__(self):
        self.y, self.x = lax.axis_index("fy"), lax.axis_index("fx")
        self.z = lax.axis_index("slot")
        self.f = 2 * self.y + self.x
        self.across_x, self.across_y = {"fx": 1 - self.x}, {"fy": 1 - self.y}
        self.c = lax.axis_index("part")
        self.above = {"slot": jnp.minimum(self.z + 1, 3)}
        self.below = {"slot": jnp.maximum(self.z - 1, 0)}
        self.batch, self.image = self.z % 2, self.z // 2
        self.mate = {"part": 1 - self.c}
        self.pair = {"slot": self.z + 1 - 2 * self.batch}
        self.cross = {"slot": self.z + 2 - 4 * self.image}

    def owned(self, segments):
        mine = segments == (self.f * 2 + self.batch) * IMG_MB + self.image
        return mine | ((segments == -1) & (self.image == 0))

    def slot_after(self, d):
        return {"slot": (self.z + d) % 4}

    def barrier(self):
        sem = pltpu.get_barrier_semaphore()
        others = [self.across_x, self.across_y, self.mate] + [self.slot_after(d) for d in (1, 2, 3)]
        for device in others:
            pl.semaphore_signal(sem, inc=1, device_id=device, device_id_type=MESH)
        pl.semaphore_wait(sem, len(others))

    def far_first(self, i):
        low = self.z < 2
        near = jnp.where(low, self.z, 3 - self.z)
        at = jnp.where(i == 0, 3, jnp.where(i == 1, 2, jnp.where(i == 2, 1 - near, near)))
        return jnp.where(low, at, 3 - at)


def send(src, dst, send_sem, recv_sem, device):
    return pltpu.make_async_remote_copy(
        src_ref=src, dst_ref=dst, send_sem=send_sem, recv_sem=recv_sem, device_id=device, device_id_type=MESH
    )


class Gather:
    SEMS = 11

    def __init__(self, place, shards, w, sems, local_sem, rows):
        self.p, self.shards, self.w, self.rows = place, shards, w, rows
        (self.zr, self.zu, self.zd, self.xr, self.xs, self.yr, self.ys, self.ar, self.asn, self.br, self.bs) = sems
        self.local_sem = local_sem

    def block(self, k, slot, owner, half=None):
        at, count = owner * self.rows, self.rows
        if half is not None:
            count = count // 2
            at = at + half * count
        return self.w[k].at[slot, pl.ds(pl.multiple_of(at, 16), count), :]

    def mine(self, k, slot, shard):
        return self.shards[k] if shard else self.block(k, slot, self.p.f)

    def up(self, k, slot, shard=False):
        dst = self.block(k, slot, self.p.f)
        return send(self.mine(k, slot, shard), dst, self.zu.at[k, slot], self.zr.at[k, slot], self.p.above)

    def down(self, k, slot, shard=False):
        dst = self.block(k, slot, self.p.f)
        return send(self.mine(k, slot, shard), dst, self.zd.at[k, slot], self.zr.at[k, slot], self.p.below)

    def to_x(self, k, slot, shard=False):
        dst = self.block(k, slot, self.p.f)
        return send(self.mine(k, slot, shard), dst, self.xs.at[k, slot], self.xr.at[k, slot], self.p.across_x)

    def to_y(self, k, slot, shard=False):
        dst = self.block(k, slot, self.p.f)
        return send(self.mine(k, slot, shard), dst, self.ys.at[k, slot], self.yr.at[k, slot], self.p.across_y)

    def from_x(self, k, slot):
        ref = self.block(k, slot, self.p.f ^ 1)
        return send(ref, ref, self.xs.at[k, slot], self.xr.at[k, slot], self.p.across_x)

    def from_y(self, k, slot):
        ref = self.block(k, slot, self.p.f ^ 2)
        return send(ref, ref, self.ys.at[k, slot], self.yr.at[k, slot], self.p.across_y)

    def corner_y(self, k, slot):
        ref = self.block(k, slot, self.p.f ^ 1, 0)
        return send(ref, ref, self.asn.at[k, slot], self.ar.at[k, slot], self.p.across_y)

    def corner_x(self, k, slot):
        ref = self.block(k, slot, self.p.f ^ 2, 1)
        return send(ref, ref, self.bs.at[k, slot], self.br.at[k, slot], self.p.across_x)

    def wait_corner(self, k, slot):
        ref = self.block(k, slot, self.p.f ^ 3, 0)
        send(ref, ref, self.asn.at[k, slot], self.ar.at[k, slot], self.p.across_y).wait_recv()
        ref = self.block(k, slot, self.p.f ^ 3, 1)
        send(ref, ref, self.bs.at[k, slot], self.br.at[k, slot], self.p.across_x).wait_recv()

    def local(self, k):
        return pltpu.make_async_copy(self.shards[k], self.block(k, self.p.z, self.p.f), self.local_sem.at[k])

    def start_z(self, k):
        @pl.when(self.p.z < 3)
        def _():
            self.up(k, self.p.z, True).start()

        @pl.when(self.p.z > 0)
        def _():
            self.down(k, self.p.z, True).start()

    def start_xy(self, k):
        self.to_x(k, self.p.z, True).start()
        self.to_y(k, self.p.z, True).start()
        self.local(k).start()

    def pass_on(self, k, d):
        z = self.p.z

        @pl.when(z >= d)
        def _():
            self.up(k, z - d).wait_recv()

            @pl.when(z < 3)
            def _():
                self.up(k, z - d).start()

            self.to_x(k, z - d).start()
            self.to_y(k, z - d).start()

        @pl.when(z + d <= 3)
        def _():
            self.down(k, z + d).wait_recv()

            @pl.when(z > 0)
            def _():
                self.down(k, z + d).start()

            self.to_x(k, z + d).start()
            self.to_y(k, z + d).start()

    def corner(self, k, d):
        def one(slot):
            self.from_x(k, slot).wait_recv()
            self.corner_y(k, slot).start()
            self.from_y(k, slot).wait_recv()
            self.corner_x(k, slot).start()

        z = self.p.z
        if d == 0:
            one(z)
        else:
            pl.when(z >= d)(lambda: one(z - d))
            pl.when(z + d <= 3)(lambda: one(z + d))

    def arrive(self, k):
        self.local(k).wait()
        for slot in range(4):
            self.wait_corner(k, slot)

    def drain(self, k):
        z = self.p.z
        for slot in range(4):
            self.to_x(k, slot).wait_send()
            self.to_y(k, slot).wait_send()
            self.corner_y(k, slot).wait_send()
            self.corner_x(k, slot).wait_send()

            @pl.when((z < 3) & (slot <= z))
            def _(slot=slot):
                self.up(k, slot).wait_send()

            @pl.when((z > 0) & (slot >= z))
            def _(slot=slot):
                self.down(k, slot).wait_send()


def gather_weights(shards):
    slots = lax.axis_size("slot")
    whole = [lax.all_gather(s, ("slot",) + FSDP, axis=0) for s in shards]
    return [w.reshape(slots, -1, w.shape[-1]) for w in whole]


class Rows:
    SEMS = 11

    def __init__(self, place, index, src, dst, sems, rows_each, edge, tail):
        self.p, self.src, self.dst, self.each = place, src, dst, rows_each
        self.half = 4 * rows_each
        self.edge, self.tail = edge, tail
        self.sems = [sem.at[index] for sem in sems]

    def at(self, row, count):
        return self.dst.at[pl.ds(pl.multiple_of(row, 16), count), :]

    def block(self, near, core):
        batch = self.p.batch if near else 1 - self.p.batch
        return self.at((2 * batch + core) * self.each, self.each)

    def own(self):
        return pltpu.make_async_copy(self.src.at[self.p.batch], self.block(True, self.p.c), self.sems[0])

    def to_mate(self):
        return send(self.src.at[self.p.batch], self.block(True, self.p.c), self.sems[1], self.sems[2], self.p.mate)

    def to_pair(self):
        return send(self.src.at[1 - self.p.batch], self.block(True, self.p.c), self.sems[3], self.sems[4], self.p.pair)

    def pass_on(self):
        ref = self.block(False, self.p.c)
        return send(ref, ref, self.sems[5], self.sems[6], self.p.mate)

    def edge_out(self):
        src = self.at(jnp.where(self.p.image == 0, self.half - self.edge, 0), self.edge)
        return send(src, self.at(self.half, self.edge), self.sems[7], self.sems[8], self.p.cross)

    def tail_out(self):
        src = self.at(self.half - self.tail, self.tail)
        dst = self.at(self.half + self.edge, self.tail)
        return send(src, dst, self.sems[7], self.sems[8], self.p.cross)

    def edge_mate(self):
        ref = self.at(self.half, self.edge)
        return send(ref, ref, self.sems[9], self.sems[10], self.p.mate)

    def tail_mate(self):
        ref = self.at(self.half + self.edge, self.tail)
        return send(ref, ref, self.sems[9], self.sems[10], self.p.mate)

    def start(self):
        self.to_pair().start()
        self.to_mate().start()
        self.own().start()

    def forward(self):
        ref = self.block(False, self.p.c)
        send(ref, ref, self.sems[3], self.sems[4], self.p.pair).wait_recv()
        self.pass_on().start()

    def main_ready(self):
        self.own().wait()
        ref = self.block(True, 1 - self.p.c)
        send(ref, ref, self.sems[1], self.sems[2], self.p.mate).wait_recv()
        ref = self.block(False, 1 - self.p.c)
        send(ref, ref, self.sems[5], self.sems[6], self.p.mate).wait_recv()

    def edges(self):
        pl.when(self.p.c == 0)(lambda: self.edge_out().start())
        pl.when(self.p.c == 1)(lambda: self.tail_out().start())

    def edges_forward(self):
        @pl.when(self.p.c == 0)
        def _():
            self.edge_out().wait_recv()
            self.edge_mate().start()

        @pl.when(self.p.c == 1)
        def _():
            self.tail_out().wait_recv()
            self.tail_mate().start()

    def edges_ready(self):
        pl.when(self.p.c == 0)(lambda: self.tail_mate().wait_recv())
        pl.when(self.p.c == 1)(lambda: self.edge_mate().wait_recv())

    def drain(self):
        self.to_mate().wait_send()
        self.to_pair().wait_send()
        self.pass_on().wait_send()

        @pl.when(self.p.c == 0)
        def _():
            self.edge_out().wait_send()
            self.edge_mate().wait_send()

        @pl.when(self.p.c == 1)
        def _():
            self.tail_out().wait_send()
            self.tail_mate().wait_send()


def row_tiles(rows, step, body):
    def one(t, carry):
        body(pl.ds(pl.multiple_of(t * step, 16), step))
        return carry

    lax.fori_loop(0, rows // step, one, 0)


def forward_kernel(*refs, cols, unit_rest, edge, tail, tile):
    (in_ref, out_ref, up_whole, down_whole, qv_ref, unit_ref, x_src, c_src, gain_ref, shift_ref, segc_ref) = refs[:11]
    segr_ref, refs = refs[11], refs[1:]
    (ws, wu, wd, gd) = refs[11:15]
    outs, refs = refs[15:29], refs[29:]
    held, refs = refs[:14], refs[14:]
    (x_ref, c_ref, first_ref, qkv_ref, ctx_ref, inv_ref, res_ref, second_ref) = held[:8]
    (hidden_ref, slope_ref, hidden_rest, slope_rest, rest_up, rest_down) = held[8:]
    (blocks, unit_blocks, grads, part, part_out, part_in, bias_rest, vec_all) = refs[:8]
    (small_ref, up_ref, down_ref, vec_ref) = refs[8:12]
    gather_sems, local_sem = refs[12 : 12 + Gather.SEMS], refs[12 + Gather.SEMS]
    tail_refs = refs[13 + Gather.SEMS :]
    row_sems = tail_refs[: Rows.SEMS]
    (vec_s, vec_r, load_sem, part_s, part_r, unit_sem, grad_sem, out_sem) = tail_refs[Rows.SEMS :]

    def leave(n):
        return pltpu.make_async_copy(held[n], outs[n], out_sem.at[n])

    main, rest = up_ref.shape[1], unit_rest
    rows, width = x_ref.shape
    place = Place()
    for n in range(3):
        small_ref[:, n * cols : (n + 1) * cols] = in_ref[n]
    at = 3 * cols
    small_ref[:, at : at + cols] = out_ref[...].T
    at = at + cols
    small_ref[:, at : at + rest] = up_whole[:, main:]
    small_ref[:, at + rest : at + 2 * rest] = down_whole[main:, :].T
    at = at + 2 * rest
    if at < small_ref.shape[1]:
        small_ref[:, at:] = jnp.zeros((small_ref.shape[0], small_ref.shape[1] - at), BF16)
    vec_ref[...] = jnp.zeros_like(vec_ref)
    for n in (0, 1):
        high = qv_ref[n : n + 1, :].astype(BF16)
        lo = 2 * n * cols
        vec_ref[0:1, lo : lo + cols] = high
        vec_ref[1:2, lo : lo + cols] = (qv_ref[n : n + 1, :] - high.astype(F32)).astype(BF16)
    vec_ref[2:3, : main + rest] = unit_ref[...]
    place.barrier()
    shards = (small_ref, up_ref, down_ref)
    g = Gather(place, shards, (ws, wu, wd), gather_sems, local_sem, small_ref.shape[0])
    each = x_src.shape[1]
    x_rows = Rows(place, 0, x_src, x_ref, row_sems, each, edge, tail)
    c_rows = Rows(place, 1, c_src, c_ref, row_sems, each, edge, tail)

    def vec_to(d):
        device = place.slot_after(d)
        return send(vec_ref, vec_all.at[place.z], vec_s.at[d], vec_r.at[d], device)

    def vec_from(d):
        ref = vec_all.at[(place.z + 4 - d) % 4]
        return send(ref, ref, vec_s.at[d], vec_r.at[d], place.slot_after(d))

    g.start_z(0)
    g.start_xy(0)
    for d in (1, 2, 3):
        vec_to(d).start()
    x_rows.start()
    vec_all[place.z] = vec_ref[...]
    up_ref[...] = up_whole[:, :main]
    down_ref[...] = down_whole[:main, :].T
    g.pass_on(0, 1)
    g.corner(0, 0)
    x_rows.forward()
    g.pass_on(0, 2)
    x_rows.main_ready()
    x_rows.edges()
    g.corner(0, 1)
    x_rows.edges_forward()
    g.pass_on(0, 3)
    g.start_z(1)
    x_rows.edges_ready()

    def first(span):
        value = x_ref[span, :].astype(F32)
        out, _, _ = norm_forward(value, gain_ref[0:1, :], shift_ref[0:1, :])
        first_ref[span, :] = out.astype(BF16)

    row_tiles(rows, 128, first)
    leave(0).start()
    g.corner(0, 2)
    g.corner(0, 3)
    leave(2).start()
    for d in (1, 2, 3):
        vec_from(d).wait_recv()
    g.arrive(0)

    later = []
    for k in (1, 2):
        later.append(lambda k=k: g.start_xy(k))
        if k == 1:
            later.append(lambda: c_rows.start())
        for d in (1, 2, 3):
            later.append(lambda k=k, d=d: g.pass_on(k, d))
            later.append(lambda k=k, d=d: g.corner(k, d - 1))
        if k == 1:
            later.append(lambda: g.start_z(2))
            later.append(lambda: c_rows.forward())
            later.append(lambda: (c_rows.main_ready(), c_rows.edges()))
        later.append(lambda k=k: g.corner(k, 3))
        if k == 1:
            later.append(lambda: c_rows.edges_forward())

    def step(count=1):
        for _ in range(count):
            if later:
                later.pop(0)()

    step(2)

    def load(s):
        return pltpu.make_async_copy(ws.at[s], blocks.at[s % 2], load_sem.at[s % 2])

    heads = cols // DH
    rest_up[...] = jnp.zeros_like(rest_up)
    rest_down[...] = jnp.zeros_like(rest_down)
    bias_rest[...] = jnp.zeros_like(bias_rest)
    part[...] = jnp.zeros_like(part)
    load(0).start()
    points = 1 + heads
    inside = [later.pop(0) for _ in range(4 * points)]

    def at_point(s, n):
        for one in range(4):
            pl.when(s == one)(lambda one=one: inside[one * points + n]() and None)

    def one_slot(s, carry):
        load(s).wait()
        pl.when(s < 3)(lambda: load(s + 1).start())
        w = blocks.at[s % 2]
        bias = vec_all[s, 0:1, : 3 * cols].astype(F32) + vec_all[s, 1:2, : 3 * cols].astype(F32)
        projected = dot_nn(first_ref[...], w[:, : 3 * cols]) + bias
        qkv_ref[s] = projected.astype(BF16)
        at_point(s, 0)
        for head in range(heads):
            attend_head(qkv_ref, ctx_ref, inv_ref, segc_ref, segr_ref, s, head, cols, tile)
            at_point(s, 1 + head)
        part[...] += dot_nt(ctx_ref[s], w[:, 3 * cols : 4 * cols])
        at = 4 * cols
        for one in range(4):

            @pl.when(s == one)
            def _(one=one):
                rest_up[:, one * rest : (one + 1) * rest] = w[:, at : at + rest]
                rest_down[:, one * rest : (one + 1) * rest] = w[:, at + rest : at + 2 * rest]
                bias_rest[:, one * rest : (one + 1) * rest] = vec_all[one, 2:3, main : main + rest].astype(F32)

        return carry

    lax.fori_loop(0, 4, one_slot, 0)

    def halves(h):
        return pl.ds(h * (rows // 2), rows // 2)

    def exchange(h):
        src, dst = part_out.at[halves(h), :], part_in.at[halves(h), :]
        return send(src, dst, part_s.at[h], part_r.at[h], place.mate)

    for h in (0, 1):
        part_out[halves(h), :] = part[halves(h), :].astype(BF16)
        exchange(h).start()
    step()
    for n in (3, 4, 5, 12, 13):
        leave(n).start()
    for h in (0, 1):
        exchange(h).wait_recv()

    def second(span):
        value = x_ref[span, :].astype(F32) + (part_out[span, :].astype(F32) + part_in[span, :].astype(F32))
        value = value + shift_ref[2:3, :]
        res_ref[span, :] = value
        out, _, _ = norm_forward(value, gain_ref[1:2, :], shift_ref[1:2, :])
        second_ref[span, :] = out.astype(BF16)

    row_tiles(rows, 128, second)
    g.arrive(1)

    def unit_load(s):
        return pltpu.make_async_copy(wu.at[s], unit_blocks.at[s % 2], unit_sem.at[s % 2])

    unit_load(0).start()
    passing = [later.pop(0) for _ in range(4)]

    def one_block(s, carry):
        unit_load(s).wait()
        pl.when(s < 3)(lambda: unit_load(s + 1).start())
        bias = vec_all[s, 2:3, :main].astype(F32)

        def units(span):
            hidden, slope = gelu_both(dot_nn(second_ref[span, :], unit_blocks[s % 2]) + bias)
            hidden_ref[s, span, :] = hidden.astype(BF16)
            slope_ref[s, span, :] = slope.astype(BF16)

        row_tiles(rows, tile, units)
        for one in range(4):
            pl.when(s == one)(lambda one=one: passing[one]() and None)
        return carry

    lax.fori_loop(0, 4, one_block, 0)

    def units_rest(span):
        hidden, slope = gelu_both(dot_nn(second_ref[span, :], rest_up[...]) + bias_rest[...])
        hidden_rest[span, :] = hidden.astype(BF16)
        slope_rest[span, :] = slope.astype(BF16)

    for n in (6, 7):
        leave(n).start()
    row_tiles(rows, tile, units_rest)
    step()
    for n in (8, 9, 10, 11):
        leave(n).start()
    c_rows.edges_ready()
    c_rows.drain()
    c_ref[...] = jnp.where(place.owned(segc_ref[...]), c_ref[...], jnp.zeros_like(c_ref))

    def grad_out(s):
        return pltpu.make_async_copy(grads.at[s % 2], gd.at[s], grad_sem.at[s % 2])

    def down_grad(s, carry):
        pl.when(s >= 2)(lambda: grad_out(s - 2).wait())
        grads[s % 2] = dot_tn(c_ref[...], hidden_ref[s]).astype(BF16)
        grad_out(s).start()
        return carry

    lax.fori_loop(0, 2, down_grad, 0)
    step()
    lax.fori_loop(2, 4, down_grad, 0)
    step(len(later))
    leave(1).start()
    for s in (2, 3):
        grad_out(s).wait()
    g.arrive(2)
    for n in range(14):
        leave(n).wait()
    for k in (0, 1, 2):
        g.drain(k)
    x_rows.drain()
    for d in (1, 2, 3):
        vec_to(d).wait_send()
    for h in (0, 1):
        exchange(h).wait_send()


def forward_stage(
    weights, biases, x_src, c_src, gains, shifts, segc, segr, cols, units, lanes, edge, tail
):
    rows, width, shard_rows, main = segc.shape[0], x_src.shape[2], weights[2].shape[0], units // 128 * 128
    unit_rest = units - main
    heads, rest_lanes = cols // DH, round_up(4 * unit_rest, 128)
    vectors = (16, round_up(max(3 * cols, units), 128))
    vmem = pl.BlockSpec(memory_space=pltpu.VMEM)
    far = pl.BlockSpec(memory_space=pl.ANY)
    shape = jax.ShapeDtypeStruct
    dma = pltpu.SemaphoreType.DMA
    return pl.pallas_call(
        functools.partial(forward_kernel, cols=cols, unit_rest=unit_rest, edge=edge, tail=tail, tile=rows // 2),
        in_specs=[vmem] * 12,
        out_specs=[far] * 18,
        out_shape=[
            shape((4, width, lanes), BF16),
            shape((4, width, main), BF16),
            shape((4, width, main), BF16),
            shape((4, width, main), BF16),
            shape((rows, width), BF16),
            shape((rows, width), BF16),
            shape((rows, width), BF16),
            shape((4, rows, 3 * cols), BF16),
            shape((4, rows, cols), BF16),
            shape((4, rows, heads), F32),
            shape((rows, width), F32),
            shape((rows, width), BF16),
            shape((4, rows, main), BF16),
            shape((4, rows, main), BF16),
            shape((rows, rest_lanes), BF16),
            shape((rows, rest_lanes), BF16),
            shape((width, rest_lanes), BF16),
            shape((width, rest_lanes), BF16),
        ],
        scratch_shapes=[
            pltpu.VMEM((rows, width), BF16),
            pltpu.VMEM((rows, width), BF16),
            pltpu.VMEM((rows, width), BF16),
            pltpu.VMEM((4, rows, 3 * cols), BF16),
            pltpu.VMEM((4, rows, cols), BF16),
            pltpu.VMEM((4, rows, heads), F32),
            pltpu.VMEM((rows, width), F32),
            pltpu.VMEM((rows, width), BF16),
            pltpu.VMEM((4, rows, main), BF16),
            pltpu.VMEM((4, rows, main), BF16),
            pltpu.VMEM((rows, rest_lanes), BF16),
            pltpu.VMEM((rows, rest_lanes), BF16),
            pltpu.VMEM((width, rest_lanes), BF16),
            pltpu.VMEM((width, rest_lanes), BF16),
            pltpu.VMEM((2, width, lanes), BF16),
            pltpu.VMEM((2, width, main), BF16),
            pltpu.VMEM((2, width, main), BF16),
            pltpu.VMEM((rows, width), F32),
            pltpu.VMEM((rows, width), BF16),
            pltpu.VMEM((rows, width), BF16),
            pltpu.VMEM((1, rest_lanes), F32),
            pltpu.VMEM((4,) + vectors, BF16),
            pltpu.VMEM((shard_rows, lanes), BF16),
            pltpu.VMEM((shard_rows, main), BF16),
            pltpu.VMEM((shard_rows, main), BF16),
            pltpu.VMEM(vectors, BF16),
        ]
        + [dma((3, 4))] * Gather.SEMS
        + [dma((3,))]
        + [dma((2,))] * Rows.SEMS
        + [dma((4,)), dma((4,)), dma((2,)), dma((2,)), dma((2,)), dma((2,)), dma((2,)), dma((14,))],
        compiler_params=pltpu.CompilerParams(collective_id=1, has_side_effects=True, vmem_limit_bytes=64000000),
        name="forward",
    )(*weights, *biases, x_src, c_src, gains, shifts, segc, segr)


def middle_kernel(*refs, cols, unit_rest):
    (wd, wu, gd) = refs[:3]
    (hidden_far, slope_far, hidden_rest, slope_rest, rest_up, rest_down) = refs[3:9]
    (c_far, second_far, res_far, gain_ref, shift_ref) = refs[9:14]
    gu = refs[14]
    (d_out, rest_sums, half_ref, grad_ref, y_ref, sums_ref, unit_ref, unit_rest_ref) = refs[15:23]
    (blocks, grads, pre_half, part, part_out, part_in, part_in2) = refs[23:30]
    (hidden_ref, slope_ref, c_ref, second_ref, res_ref) = refs[30:35]
    d_bufs, d_own = refs[35:40], refs[40:43]
    refs = refs[43:]
    sems, loads = refs[: Reduce.SEMS], refs[Reduce.SEMS : Reduce.SEMS + 3]
    load_sem, grad_sem, part_s, part_r, in_sem, unit_sem = refs[Reduce.SEMS + 3 :]
    rows, width = c_ref.shape
    rest = unit_rest
    place = Place()
    place.barrier()

    def down_final(total):
        d_out[...] = total[...].astype(F32).T

    r = Reduce(place, (gd,), (d_own,), (down_final,), (d_bufs,), sems, loads, d_out.shape[1])

    def load(w, slot, buffer):
        return pltpu.make_async_copy(w.at[slot], blocks.at[buffer], load_sem.at[buffer])

    def halves(h):
        return pl.ds(h * (rows // 2), rows // 2)

    def exchange(n, h):
        dst = (part_in, part_in2)[n]
        src, dst = part_out.at[halves(h), :], dst.at[halves(h), :]
        return send(src, dst, part_s.at[n, h], part_r.at[n, h], place.mate)

    def enter(n):
        far, near = ((c_far, c_ref), (second_far, second_ref), (res_far, res_ref))[n]
        return pltpu.make_async_copy(far, near, in_sem.at[n])

    def unit_loads(s):
        return (
            pltpu.make_async_copy(hidden_far.at[s], hidden_ref.at[s % 2], unit_sem.at[0, s % 2]),
            pltpu.make_async_copy(slope_far.at[s], slope_ref.at[s % 2], unit_sem.at[1, s % 2]),
        )

    def start_units(s):
        for copy in unit_loads(s):
            copy.start()

    enter(0).start()
    load(wd, 0, 0).start()
    start_units(0)
    r.start(0)
    enter(1).start()
    enter(2).start()
    enter(0).wait()
    part[...] = dot_nt(hidden_rest[...], rest_down[...])
    grad_rest = slope_rest[...].astype(F32) * dot_nn(c_ref[...], rest_down[...])
    unit_rest_ref[...] = jnp.sum(grad_rest, axis=0, keepdims=True)
    half_rest = grad_rest.astype(BF16)

    def down_block(s, carry):
        load(wd, s, s % 2).wait()
        pl.when(s < 3)(lambda: load(wd, s + 1, (s + 1) % 2).start())
        pl.when(s == 3)(lambda: load(wu, 0, 0).start())
        for copy in unit_loads(s):
            copy.wait()
        pl.when(s < 3)(lambda: start_units(s + 1))
        w = blocks[s % 2]
        part[...] += dot_nt(hidden_ref[s % 2], w)
        grad = slope_ref[s % 2].astype(F32) * dot_nn(c_ref[...], w)
        pre_half[s] = grad.astype(BF16)
        unit_ref[s] = jnp.broadcast_to(jnp.sum(grad, axis=0, keepdims=True), unit_ref.shape[1:])
        r.middle_one(0, s)
        return carry

    lax.fori_loop(0, 4, down_block, 0)
    for h in (0, 1):
        part_out[halves(h), :] = part[halves(h), :].astype(BF16)
        exchange(0, h).start()
    enter(1).wait()
    enter(2).wait()
    up_sum = dot_tn(second_ref[...], half_rest).astype(BF16)
    down_sum = dot_tn(c_ref[...], hidden_rest[...]).astype(BF16)
    rest_sums[...] = jnp.zeros_like(rest_sums)
    for s in range(4):
        rest_sums[s, :, :rest] = up_sum[:, s * rest : (s + 1) * rest]
        rest_sums[s, :, rest : 2 * rest] = down_sum[:, s * rest : (s + 1) * rest]
    part[...] = dot_nt(half_rest, rest_up[...])

    def grad_out(s):
        return pltpu.make_async_copy(grads.at[s % 2], gu.at[s], grad_sem.at[s % 2])

    def up_block(s, carry):
        load(wu, s, s % 2).wait()
        pl.when(s < 3)(lambda: load(wu, s + 1, (s + 1) % 2).start())
        part[...] += dot_nt(pre_half[s], blocks[s % 2])
        pl.when(s >= 2)(lambda: grad_out(s - 2).wait())
        grads[s % 2] = dot_tn(second_ref[...], pre_half[s]).astype(BF16)
        grad_out(s).start()
        pl.when(s >= 2)(lambda: r.line_one(0, s - 2))
        return carry

    lax.fori_loop(0, 4, up_block, 0)
    for h in (0, 1):
        exchange(0, h).wait_recv()

    def output(span):
        value = part_out[span, :].astype(F32) + part_in[span, :].astype(F32)
        y_ref[span, :] = (res_ref[span, :] + value + shift_ref[3:4, :]).astype(BF16)

    row_tiles(rows, 128, output)
    for h in (0, 1):
        exchange(0, h).wait_send()
        part_out[halves(h), :] = part[halves(h), :].astype(BF16)
        exchange(1, h).start()
    r.line_one(0, 2)
    r.line_one(0, 3)
    for h in (0, 1):
        exchange(1, h).wait_recv()
    sums_ref[...] = jnp.zeros_like(sums_ref)

    def back(span):
        grad = part_out[span, :].astype(F32) + part_in2[span, :].astype(F32)
        upstream = c_ref[span, :].astype(F32)
        _, scaled, factor = norm_forward(res_ref[span, :], gain_ref[1:2, :], shift_ref[1:2, :])
        value = upstream + norm_backward(grad, scaled, factor, gain_ref[1:2, :])
        grad_ref[span, :] = value
        half_ref[span, :] = value.astype(BF16)
        sums_ref[1:2, :] += jnp.sum(grad * scaled, axis=0, keepdims=True)
        sums_ref[3:4, :] += jnp.sum(grad, axis=0, keepdims=True)
        sums_ref[4:5, :] += jnp.sum(value, axis=0, keepdims=True)
        sums_ref[5:6, :] += jnp.sum(upstream, axis=0, keepdims=True)

    row_tiles(rows, 128, back)
    for s in (2, 3):
        grad_out(s).wait()
    r.drain(0)
    for h in (0, 1):
        exchange(1, h).wait_send()


def middle_stage(
    wd, wu, gd, hidden, slope, hidden_rest, slope_rest, rest_up, rest_down, cot, second, residual, gains, shifts, cols, unit_rest, spare
):
    rows, width = cot.shape
    main, shard_rows = wd.shape[2], width // 4
    vmem = pl.BlockSpec(memory_space=pltpu.VMEM)
    far = pl.BlockSpec(memory_space=pl.ANY)
    shape = jax.ShapeDtypeStruct
    dma = pltpu.SemaphoreType.DMA
    return pl.pallas_call(
        functools.partial(middle_kernel, cols=cols, unit_rest=unit_rest),
        in_specs=[far] * 5 + [vmem] * 4 + [far] * 3 + [vmem] * 2,
        out_specs=[far] + [vmem] * 8,
        out_shape=[
            shape((4, width, main), BF16),
            shape((main, shard_rows), F32),
            shape((4, width, 2 * unit_rest + spare), BF16),
            shape((rows, width), BF16),
            shape((rows, width), F32),
            shape((rows, width), BF16),
            shape((8, width), F32),
            shape((4, 8, main), F32),
            shape((1, rest_up.shape[1]), F32),
        ],
        scratch_shapes=[
            pltpu.VMEM((2, width, main), BF16),
            pltpu.VMEM((2, width, main), BF16),
            pltpu.VMEM((4, rows, main), BF16),
            pltpu.VMEM((rows, width), F32),
            pltpu.VMEM((rows, width), BF16),
            pltpu.VMEM((rows, width), BF16),
            pltpu.VMEM((rows, width), BF16),
            pltpu.VMEM((2, rows, main), BF16),
            pltpu.VMEM((2, rows, main), BF16),
            pltpu.VMEM((rows, width), BF16),
            pltpu.VMEM((rows, width), BF16),
            pltpu.VMEM((rows, width), F32),
        ]
        + reduce_buffers(shard_rows, main)
        + reduce_terms(shard_rows, main)
        + [dma((1, 4))] * Reduce.SEMS
        + [dma((1, 4))] * 3
        + [dma((2,)), dma((2,)), dma((2, 2)), dma((2, 2)), dma((3,)), dma((2, 2))],
        compiler_params=pltpu.CompilerParams(collective_id=3, has_side_effects=True, vmem_limit_bytes=64000000),
        name="middle",
    )(wd, wu, gd, hidden, slope, hidden_rest, slope_rest, rest_up, rest_down, cot, second, residual, gains, shifts)


class Reduce:
    SEMS = 16

    def __init__(self, place, g, own, out, bufs, sems, load_sems, rows):
        self.p, self.g, self.own, self.out, self.rows = place, g, own, out, rows
        self.bufs, self.sems, self.load_sems = bufs, sems, load_sems

    def grad(self, k, slot, owner, half=None):
        at, count = owner * self.rows, self.rows
        if half is not None:
            count = count // 2
            at = at + half * count
        return self.g[k].at[slot, pl.ds(pl.multiple_of(at, 16), count), :]

    def terms(self, k, slot):
        f = self.p.f
        if self.own[k] is None:
            return self.grad(k, slot, f ^ 1, 0), self.grad(k, slot, f ^ 2, 1), self.grad(k, slot, f)
        return tuple(ref.at[slot] for ref in self.own[k])

    def loads(self, k, slot):
        f = self.p.f
        src = self.grad(k, slot, f ^ 1, 0), self.grad(k, slot, f ^ 2, 1), self.grad(k, slot, f)
        pairs = zip(src, self.terms(k, slot), self.load_sems)
        return [pltpu.make_async_copy(one, dst, sem.at[k, slot]) for one, dst, sem in pairs]

    def half(self, ref, slot, half):
        count = self.rows // 2
        return ref.at[slot, half * count : (half + 1) * count, :]

    def copy(self, k, slot, src, dst, index, device):
        return send(src, dst, self.sems[2 * index].at[k, slot], self.sems[2 * index + 1].at[k, slot], device)

    def corner_y(self, k, s):
        return self.copy(k, s, self.grad(k, s, self.p.f ^ 3, 0), self.bufs[k][0].at[s], 0, self.p.across_y)

    def corner_x(self, k, s):
        return self.copy(k, s, self.grad(k, s, self.p.f ^ 3, 1), self.bufs[k][1].at[s], 1, self.p.across_x)

    def x_low(self, k, s):
        return self.copy(k, s, self.bufs[k][0].at[s], self.half(self.bufs[k][2], s, 0), 2, self.p.across_x)

    def x_high(self, k, s):
        dst = self.half(self.bufs[k][2], s, 1)
        return self.copy(k, s, self.grad(k, s, self.p.f ^ 1, 1), dst, 3, self.p.across_x)

    def y_low(self, k, s):
        dst = self.half(self.bufs[k][3], s, 0)
        return self.copy(k, s, self.grad(k, s, self.p.f ^ 2, 0), dst, 4, self.p.across_y)

    def y_high(self, k, s):
        return self.copy(k, s, self.bufs[k][1].at[s], self.half(self.bufs[k][3], s, 1), 5, self.p.across_y)

    def up(self, k, s):
        return self.copy(k, s, self.bufs[k][2].at[s], self.bufs[k][4].at[s], 6, self.p.above)

    def down(self, k, s):
        at = jnp.where(s == self.p.z - 1, 4, s)
        return self.copy(k, s, self.bufs[k][2].at[s], self.bufs[k][4].at[at], 7, self.p.below)

    def from_above(self, k, s):
        at = jnp.where(s == self.p.z, 4, s)
        return self.copy(k, s, self.bufs[k][4].at[at], self.bufs[k][4].at[at], 7, self.p.below), at

    def start_one(self, k, s):
        self.corner_y(k, s).start()
        self.corner_x(k, s).start()
        self.y_low(k, s).start()
        self.x_high(k, s).start()

    def start(self, k):
        def one(i, carry):
            self.start_one(k, self.p.far_first(i))
            return carry

        lax.fori_loop(0, 4, one, 0)
        if self.own[k] is not None:
            for slot in range(4):
                for load in self.loads(k, slot):
                    load.start()

    def tiles(self, rows, body):
        row_tiles(rows, 48 if rows % 48 == 0 else 16, body)

    def middle_one(self, k, i):
        s, count = self.p.far_first(i), self.rows // 2
        low, high = self.bufs[k][0], self.bufs[k][1]
        if self.own[k] is not None:
            for load in self.loads(k, s):
                load.wait()
        own_low, own_high, _ = self.terms(k, s)
        self.corner_y(k, s).wait_recv()

        def add_low(span):
            low[s, span, :] = add_half(low[s, span, :], own_low[span, :])

        self.tiles(count, add_low)
        self.corner_x(k, s).wait_recv()

        def add_high(span):
            high[s, span, :] = add_half(high[s, span, :], own_high[span, :])

        self.tiles(count, add_high)
        self.x_low(k, s).start()
        self.y_high(k, s).start()

    def line_one(self, k, i):
        z, acc, side, far = self.p.z, self.bufs[k][2], self.bufs[k][3], self.bufs[k][4]
        s = self.p.far_first(i)
        self.x_low(k, s).wait_recv()
        self.x_high(k, s).wait_recv()
        self.y_low(k, s).wait_recv()
        self.y_high(k, s).wait_recv()
        own = self.terms(k, s)[2]

        def add(span):
            total = own[span, :].astype(F32) + acc[s, span, :].astype(F32) + side[s, span, :].astype(F32)
            acc[s, span, :] = total.astype(BF16)

        self.tiles(self.rows, add)

        def add_far(at):
            def body(span):
                acc[s, span, :] = add_half(acc[s, span, :], far[at, span, :])

            self.tiles(self.rows, body)

        @pl.when((z > 0) & (s >= z))
        def _():
            self.up(k, s).wait_recv()
            add_far(s)

        @pl.when((z < 3) & (s <= z))
        def _():
            copy, at = self.from_above(k, s)
            copy.wait_recv()
            add_far(at)

        @pl.when(s > z)
        def _():
            self.up(k, s).start()

        @pl.when(s < z)
        def _():
            self.down(k, s).start()

        @pl.when(s == z)
        def _():
            self.out[k](acc.at[s])

    def loop(self, one):
        def body(i, carry):
            one(i)
            return carry

        lax.fori_loop(0, 4, body, 0)

    def drain(self, k):
        def one(s):
            for copy in (self.corner_y, self.corner_x, self.x_low, self.x_high, self.y_low, self.y_high):
                copy(k, s).wait_send()

            @pl.when(s > self.p.z)
            def _():
                self.up(k, s).wait_send()

            @pl.when(s < self.p.z)
            def _():
                self.down(k, s).wait_send()

        self.loop(one)


def reduce_buffers(rows, lanes):
    half, whole = pltpu.VMEM((4, rows // 2, lanes), BF16), pltpu.VMEM((4, rows, lanes), BF16)
    return [half, half, whole, whole, pltpu.VMEM((5, rows, lanes), BF16)]


def reduce_terms(rows, lanes):
    half, whole = pltpu.VMEM((4, rows // 2, lanes), BF16), pltpu.VMEM((4, rows, lanes), BF16)
    return [half, half, whole]


def scatter_grads(chunks):
    count = lax.axis_size("fy") * lax.axis_size("fx")
    split = [c.reshape(c.shape[0] * count, c.shape[1] // count, c.shape[2]) for c in chunks]
    return [lax.psum_scatter(c, ("slot",) + FSDP, scatter_dimension=0).astype(F32) for c in split]


class RowsBack:
    SEMS = 7

    def __init__(self, place, index, window, inbox, owned, out, sems, rows_each, edge, tail):
        self.p, self.window, self.inbox, self.owned, self.out = place, window, inbox, owned, out
        self.each, self.half, self.edge, self.tail = rows_each, 4 * rows_each, edge, tail
        self.sems = [sem.at[index] for sem in sems]

    def edge_out(self):
        src = self.window.at[self.half : self.half + self.edge, :]
        return send(src, self.inbox.at[: self.edge, :], self.sems[0], self.sems[1], self.p.cross)

    def tail_out(self):
        src = self.window.at[self.half + self.edge :, :]
        return send(src, self.inbox.at[self.edge :, :], self.sems[2], self.sems[3], self.p.cross)

    def block(self, near):
        batch = self.p.batch if near else 1 - self.p.batch
        row = (2 * batch + self.p.c) * self.each
        return self.window.at[pl.ds(pl.multiple_of(row, 16), self.each), :]

    def stay(self):
        return pltpu.make_async_copy(self.block(True), self.out.at[self.p.batch], self.sems[4])

    def to_pair(self):
        return send(self.block(False), self.out.at[self.p.batch], self.sems[5], self.sems[6], self.p.pair)

    def edges(self):
        pl.when(self.p.c == self.p.image)(lambda: self.edge_out().start())
        pl.when((self.p.c == 1) & (self.p.image == 0))(lambda: self.tail_out().start())

    def merge(self, row, count, at):
        keep = self.p.owned(self.owned[row : row + count, :])
        value = jnp.where(keep, self.window[row : row + count, :], self.inbox[at : at + count, :])
        self.window[row : row + count, :] = value

    def finish(self):
        p = self.p

        @pl.when((p.c == 1) & (p.image == 0))
        def _():
            self.edge_out().wait_recv()
            self.merge(self.half - self.edge, self.edge, 0)

        @pl.when((p.c == 0) & (p.image == 1))
        def _():
            self.edge_out().wait_recv()
            self.merge(0, self.edge, 0)

        @pl.when((p.c == 1) & (p.image == 1))
        def _():
            self.tail_out().wait_recv()
            self.merge(self.half - self.tail, self.tail, self.edge)

        self.to_pair().start()
        self.stay().start()

    def drain(self):
        pl.when(self.p.c == self.p.image)(lambda: self.edge_out().wait_send())
        pl.when((self.p.c == 1) & (self.p.image == 0))(lambda: self.tail_out().wait_send())
        self.stay().wait()
        self.to_pair().wait_send()
        ref = self.out.at[1 - self.p.batch]
        send(ref, ref, self.sems[5], self.sems[6], self.p.pair).wait_recv()


def backward_kernel(*refs, cols, unit_rest, edge, tail, tile):
    (ws, gu, rest_ref, half_ref, first_far, qkv_far, ctx_far, inv_far, segc_ref, segr_whole) = refs[:10]
    (x_far, res_grad_ref, y_ref, gain_ref, d_in, old_sums, unit_ref, unit_rest_ref) = refs[10:18]
    (in_out, out_out, up_out, down_out, x_final, y_out, gain_out, shift_out, qv_out, unit_out) = refs[18:28]
    refs = refs[28:]
    (segr_ref, x_out, sums_ref), refs = refs[:3], refs[3:]
    (blocks, gs, part, part_out, part_in, back_ref, grad_ref, key_acc, value_acc, inbox_x, inbox_y) = refs[:11]
    y_window = part_out
    bias_ref, sums_in, vec_sum, vec_in, vec_far = refs[11:16]
    first_ref, qkv_ref, ctx_ref, inv_ref, x_ref = refs[16:21]
    u_bufs, s_bufs, u_own = refs[21:26], refs[26:31], refs[31:34]
    refs = refs[34:]
    sems, loads, back_sems = refs[: Reduce.SEMS], refs[Reduce.SEMS : Reduce.SEMS + 3], refs[Reduce.SEMS + 3 : Reduce.SEMS + 3 + RowsBack.SEMS]
    load_sem, part_s, part_r, y_sems, sum_s, sum_r, vec_s, vec_r, in_sem = refs[Reduce.SEMS + 3 + RowsBack.SEMS :]
    rows, width = half_ref.shape
    shard_rows, main, rest = up_out.shape[0], gu.shape[2], unit_rest
    heads = cols // DH
    place = Place()
    place.barrier()
    each = x_out.shape[1]

    def up_final(total):
        up_out[:, :main] = total[...].astype(F32)

    def small_final(total):
        for n in range(3):
            in_out[n] = total[:, n * cols : (n + 1) * cols].astype(F32)
        at = 3 * cols
        out_out[...] = total[:, at : at + cols].astype(F32).T
        at = at + cols
        up_out[:, main:] = total[:, at : at + rest].astype(F32)
        down_out[main:, :] = total[:, at + rest : at + 2 * rest].astype(F32).T

    r = Reduce(place, (gu, gs), (u_own, None), (up_final, small_final), (u_bufs, s_bufs), sems, loads, shard_rows)
    x_back = RowsBack(place, 0, part_in, inbox_x, segc_ref, x_out, back_sems, each, edge, tail)
    y_back = RowsBack(place, 1, y_window, inbox_y, segc_ref, y_out, back_sems, each, edge, tail)

    def load(i):
        return pltpu.make_async_copy(ws.at[place.far_first(i)], blocks.at[i % 2], load_sem.at[i % 2])

    y_load = pltpu.make_async_copy(y_ref, y_window, y_sems.at[0])
    def slot_loads(i):
        s = place.far_first(i)
        pairs = ((qkv_far, qkv_ref), (ctx_far, ctx_ref), (inv_far, inv_ref))
        return [pltpu.make_async_copy(p[0].at[s], p[1].at[s], in_sem.at[n, i]) for n, p in enumerate(pairs)]

    first_load = pltpu.make_async_copy(first_far, first_ref, y_sems.at[1])
    x_load = pltpu.make_async_copy(x_far, x_ref, y_sems.at[2])
    load(0).start()
    for copy in slot_loads(0):
        copy.start()
    y_load.start()
    r.start(0)
    for t in range(rows // tile):
        segr_ref[t] = segr_whole[:, t * tile : (t + 1) * tile]
    down_out[:main, :] = d_in[...]
    first_load.start()
    for i in (1, 2, 3):
        for copy in slot_loads(i):
            copy.start()
    x_load.start()
    y_load.wait()
    y_back.edges()

    def one_slot(i, carry):
        s = place.far_first(i)
        load(i).wait()
        for copy in slot_loads(i):
            copy.wait()

        @pl.when(i < 3)
        def _():
            load(i + 1).start()

        w = blocks.at[i % 2]
        back_ref[...] = dot_nn(half_ref[...], w[:, 3 * cols : 4 * cols]).astype(BF16)
        gs[s, :, 3 * cols : 4 * cols] = dot_tn(half_ref[...], ctx_ref[s]).astype(BF16)
        gs[s, :, 4 * cols :] = rest_ref[s]
        for head in range(heads):
            attend_back_head(
                qkv_ref, ctx_ref, inv_ref, back_ref, segc_ref, segr_ref, grad_ref, bias_ref, key_acc, value_acc, s, head, cols, tile
            )
            if head == 0:
                r.middle_one(0, i)
                pl.when(i == 1)(lambda: y_back.finish())
        pl.when(i == 0)(lambda: first_load.wait())
        gs[s, :, : 3 * cols] = dot_tn(first_ref[...], grad_ref[...]).astype(BF16)
        product = dot_nt(grad_ref[...], w[:, : 3 * cols])

        @pl.when(i == 0)
        def _():
            part[...] = product

        @pl.when(i > 0)
        def _():
            part[...] += product

        r.start_one(1, s)
        pl.when(i > 0)(lambda: r.line_one(0, i - 1))
        pl.when(i > 0)(lambda: r.middle_one(1, i - 1))
        return carry

    lax.fori_loop(0, 4, one_slot, 0)

    def halves(h):
        return pl.ds(h * (rows // 2), rows // 2)

    def exchange(h):
        src, dst = part_out.at[halves(h), :], part_in.at[halves(h), :]
        return send(src, dst, part_s.at[h], part_r.at[h], place.mate)

    y_back.drain()
    for h in (0, 1):
        part_out[halves(h), :] = part[halves(h), :].astype(BF16)
        exchange(h).start()
    res_load = pltpu.make_async_copy(res_grad_ref, part, load_sem.at[0])
    res_load.start()
    r.line_one(0, 3)
    pl.when((place.z == 0) | (place.z == 3))(lambda: r.line_one(1, 0))
    for h in (0, 1):
        exchange(h).wait_recv()

    res_load.wait()
    x_load.wait()
    sums_ref[...] = old_sums[...]

    def last(span):
        grad = part_out[span, :].astype(F32) + part_in[span, :].astype(F32)
        value = x_ref[span, :].astype(F32)
        _, scaled, factor = norm_forward(value, gain_ref[0:1, :], gain_ref[0:1, :])
        result = part[span, :] + norm_backward(grad, scaled, factor, gain_ref[0:1, :])
        part_in[span, :] = result.astype(BF16)
        sums_ref[0:1, :] += jnp.sum(grad * scaled, axis=0, keepdims=True)
        sums_ref[2:3, :] += jnp.sum(grad, axis=0, keepdims=True)

    row_tiles(rows, 128, last)
    x_back.edges()

    vec_sum[...] = jnp.zeros_like(vec_sum)
    for s in range(4):
        vec_sum[s, 0:1, :cols] = bias_ref[s, 0:1, :]
        vec_sum[s, 1:2, :cols] = bias_ref[s, 1:2, :]
        vec_sum[s, 2:3, :main] = unit_ref[s, 0:1, :]
        vec_sum[s, 3:4, :rest] = unit_rest_ref[:, s * rest : (s + 1) * rest]

    def across(n, device):
        return (
            send(sums_ref, sums_in.at[n], sum_s.at[n], sum_r.at[n], device),
            send(vec_sum, vec_in.at[n], vec_s.at[n], vec_r.at[n], device),
        )

    def along(d):
        there = (place.z + d) % 4
        device = place.slot_after(d)
        return (
            send(sums_ref, sums_in.at[1 + d], sum_s.at[1 + d], sum_r.at[1 + d], device),
            send(vec_sum.at[there], vec_far.at[d - 1], vec_s.at[1 + d], vec_r.at[1 + d], device),
        )

    def add_across(n, device):
        for copy in across(n, device):
            copy.wait()
        sums_ref[...] += sums_in[n]
        vec_sum[...] += vec_in[n]

    for copy in across(0, place.across_x):
        copy.start()
    r.middle_one(1, 3)
    pl.when((place.z == 1) | (place.z == 2))(lambda: r.line_one(1, 0))
    r.line_one(1, 1)
    add_across(0, place.across_x)
    for copy in across(1, place.across_y):
        copy.start()
    x_back.finish()
    r.line_one(1, 2)
    add_across(1, place.across_y)
    for d in (1, 2, 3):
        for copy in along(d):
            copy.start()
    r.line_one(1, 3)
    for d in (1, 2, 3):
        for copy in along(d):
            copy.wait()
    sums_ref[...] += sums_in[2] + sums_in[3] + sums_in[4]
    gain_out[...] = sums_ref[0:2, :]
    shift_out[...] = sums_ref[2:6, :]
    total = vec_sum[place.z] + vec_far[0] + vec_far[1] + vec_far[2]
    qv_out[...] = total[0:2, :cols]
    unit_out[:, :main] = total[2:3, :main]
    unit_out[:, main:] = total[3:4, :rest]
    for k in (0, 1):
        r.drain(k)
    x_back.drain()
    x_final[...] = x_out[...].astype(F32)
    for h in (0, 1):
        exchange(h).wait_send()


def backward_stage(
    ws, gu, rest_sums, residual_half, first_norm, qkv, context, inverse, segc, segr, x_half, residual_grad, y_rows, gains, down_sum,
    sums, unit_sums, unit_rest_sums, cols, unit_rest, edge, tail, rows_each,
):
    rows, width = residual_half.shape
    shard_rows, lanes, main = width // 4, ws.shape[2], gu.shape[2]
    vmem = pl.BlockSpec(memory_space=pltpu.VMEM)
    far = pl.BlockSpec(memory_space=pl.ANY)
    shape = jax.ShapeDtypeStruct
    dma = pltpu.SemaphoreType.DMA
    wide = max(main, round_up(cols, 128))
    return pl.pallas_call(
        functools.partial(backward_kernel, cols=cols, unit_rest=unit_rest, edge=edge, tail=tail, tile=rows // 2),
        in_specs=[far] * 2 + [vmem] * 2 + [far] * 4 + [vmem] * 2 + [far] * 3 + [vmem] * 5,
        out_specs=[vmem] * 10,
        out_shape=[
            shape((3, shard_rows, cols), F32),
            shape((cols, shard_rows), F32),
            shape((shard_rows, main + unit_rest), F32),
            shape((main + unit_rest, shard_rows), F32),
            shape((2, rows_each, width), F32),
            shape((2, rows_each, width), BF16),
            shape((2, width), F32),
            shape((4, width), F32),
            shape((2, cols), F32),
            shape((1, main + unit_rest), F32),
        ],
        scratch_shapes=[
            pltpu.VMEM((2, 1, rows // 2), jnp.int32),
            pltpu.VMEM((2, rows_each, width), BF16),
            pltpu.VMEM((8, width), F32),
            pltpu.VMEM((2, width, lanes), BF16),
            pltpu.VMEM((4, width, lanes), BF16),
            pltpu.VMEM((rows, width), F32),
            pltpu.VMEM((rows, width), BF16),
            pltpu.VMEM((rows, width), BF16),
            pltpu.VMEM((rows, cols), BF16),
            pltpu.VMEM((rows, 3 * cols), BF16),
            pltpu.VMEM((rows, DH), F32),
            pltpu.VMEM((rows, DH), F32),
            pltpu.VMEM((edge + tail, width), BF16),
            pltpu.VMEM((edge + tail, width), BF16),
            pltpu.VMEM((4, 2, cols), F32),
            pltpu.VMEM((5, 8, width), F32),
            pltpu.VMEM((4, 8, wide), F32),
            pltpu.VMEM((2, 4, 8, wide), F32),
            pltpu.VMEM((3, 8, wide), F32),
            pltpu.VMEM((rows, width), BF16),
            pltpu.VMEM((4, rows, 3 * cols), BF16),
            pltpu.VMEM((4, rows, cols), BF16),
            pltpu.VMEM((4, rows, cols // DH), F32),
            pltpu.VMEM((rows, width), BF16),
        ]
        + reduce_buffers(shard_rows, main)
        + reduce_buffers(shard_rows, lanes)
        + reduce_terms(shard_rows, main)
        + [dma((2, 4))] * Reduce.SEMS
        + [dma((1, 4))] * 3
        + [dma((2,))] * RowsBack.SEMS
        + [dma((2,)), dma((2,)), dma((2,)), dma((3,)), dma((5,)), dma((5,)), dma((5,)), dma((5,)), dma((3, 4))],
        compiler_params=pltpu.CompilerParams(collective_id=2, has_side_effects=True, vmem_limit_bytes=64000000),
        name="backward",
    )(
        ws, gu, rest_sums, residual_half, first_norm, qkv, context, inverse, segc, segr,
        x_half, residual_grad, y_rows, gains, down_sum, sums, unit_sums, unit_rest_sums,
    )


def attend_head(qkv_ref, ctx_ref, inv_ref, segc_ref, segr_ref, s, head, cols, tile):
    lo = head * DH
    keys = qkv_ref[s, :, cols + lo : cols + lo + DH]
    values = qkv_ref[s, :, 2 * cols + lo : 2 * cols + lo + DH]

    def one_tile(t, carry):
        span = pl.ds(pl.multiple_of(t * tile, tile), tile)
        scores = dot_nt(qkv_ref[s, span, lo : lo + DH], keys)
        allowed = segc_ref[span, :] == segr_ref[...]
        exact = jnp.where(allowed, jnp.exp2(scores * (SCALE * LOG2E)), 0.0)
        inverse = 1.0 / jnp.sum(exact, axis=1, keepdims=True)
        context = dot_nn(exact.astype(BF16), values) * inverse
        ctx_ref[s, span, lo : lo + DH] = context.astype(BF16)
        inv_ref[s, span, head : head + 1] = inverse
        return carry

    lax.fori_loop(0, qkv_ref.shape[1] // tile, one_tile, 0)


def attend_kernel(x_ref, w_ref, b_ref, segc_ref, segr_ref, qkv_ref, ctx_ref, inv_ref, part_ref, *, cols, tile):
    block = pl.program_id(0)
    projected = dot_nn(x_ref[...], w_ref[0, :, : 3 * cols]) + b_ref[0]
    qkv_ref[0] = projected.astype(BF16)
    for head in range(cols // DH):
        attend_head(qkv_ref, ctx_ref, inv_ref, segc_ref, segr_ref, 0, head, cols, tile)
    part = dot_nt(ctx_ref[0], w_ref[0, :, 3 * cols : 4 * cols])

    @pl.when(block == 0)
    def _():
        part_ref[...] = part

    @pl.when(block > 0)
    def _():
        part_ref[...] += part


def attend(first_norm, weights, bias, segments, cols, tile):
    rows, width = first_norm.shape
    slots, _, lanes = weights.shape
    heads = cols // DH
    whole = lambda shape: pl.BlockSpec(shape, lambda s: (0,) * len(shape))
    each = lambda shape: pl.BlockSpec((1,) + shape, lambda s: (s, 0, 0))
    return pl.pallas_call(
        functools.partial(attend_kernel, cols=cols, tile=tile),
        grid=(slots,),
        in_specs=[
            whole((rows, width)),
            each((width, lanes)),
            each((1, 3 * cols)),
            whole((rows, 1)),
            whole((1, rows)),
        ],
        out_specs=[each((rows, 3 * cols)), each((rows, cols)), each((rows, heads)), whole((rows, width))],
        out_shape=[
            jax.ShapeDtypeStruct((slots, rows, 3 * cols), BF16),
            jax.ShapeDtypeStruct((slots, rows, cols), BF16),
            jax.ShapeDtypeStruct((slots, rows, heads), F32),
            jax.ShapeDtypeStruct((rows, width), F32),
        ],
        cost_estimate=pl.CostEstimate(
            flops=slots * (8 * rows * width * cols + 4 * rows * rows * 256 * heads),
            bytes_accessed=slots * width * lanes * 2 + rows * width * 10,
            transcendentals=slots * heads * rows * rows,
        ),
        name="attend",
    )(first_norm, weights, bias, segments[:, None], segments[None, :])


def attend_back_head(
    qkv_ref, ctx_ref, inv_ref, back_ref, segc_ref, segr_ref, grad_ref, bias_ref, key_acc, value_acc, s, head, cols, tile
):
    lo = head * DH
    rows = back_ref.shape[0]
    ones = jnp.ones((8, DH), F32)
    keys = qkv_ref[s, :, cols + lo : cols + lo + DH]
    values = qkv_ref[s, :, 2 * cols + lo : 2 * cols + lo + DH]
    key_acc[...] = jnp.zeros_like(key_acc)
    value_acc[...] = jnp.zeros_like(value_acc)

    def one_tile(t, query_total):
        span = pl.ds(pl.multiple_of(t * tile, tile), tile)
        queries = qkv_ref[s, span, lo : lo + DH]
        back = (back_ref[span, lo : lo + DH].astype(F32) * inv_ref[s, span, head : head + 1]).astype(BF16)
        along = back.astype(F32) * ctx_ref[s, span, lo : lo + DH].astype(F32)
        delta = lax.dot_general(
            ones, along, (((1,), (1,)), ((), ())), precision=lax.Precision.HIGHEST, preferred_element_type=F32
        )[:1]
        scores = dot_nt(keys, queries)
        allowed = segc_ref[...] == segr_ref[t]
        exact = jnp.where(allowed, jnp.exp2(scores * (SCALE * LOG2E)), 0.0)
        value_acc[...] += dot_nn(exact.astype(BF16), back)
        prob_grad = dot_nt(values, back)
        score_grad = (exact * (prob_grad - delta)).astype(BF16)
        key_acc[...] += dot_nn(score_grad, queries)
        query_grad = dot_tn(score_grad, keys) * SCALE
        grad_ref[span, lo : lo + DH] = query_grad.astype(BF16)
        return query_total + jnp.sum(query_grad, axis=0, keepdims=True)

    query_total = lax.fori_loop(0, rows // tile, one_tile, jnp.zeros((1, DH), F32))
    grad_ref[:, cols + lo : cols + lo + DH] = (key_acc[...] * SCALE).astype(BF16)
    grad_ref[:, 2 * cols + lo : 2 * cols + lo + DH] = value_acc[...].astype(BF16)
    bias_ref[s, 0:1, lo : lo + DH] = query_total
    bias_ref[s, 1:2, lo : lo + DH] = jnp.sum(value_acc[...], axis=0, keepdims=True)


def attend_back_kernel(
    r_ref, w_ref, qkv_ref, ctx_ref, inv_ref, segc_ref, segr_ref, grad_ref, bias_ref, back_ref, key_acc, value_acc, *, cols, tile
):
    back_ref[...] = dot_nn(r_ref[...], w_ref[0, :, 3 * cols : 4 * cols]).astype(BF16)
    for head in range(cols // DH):
        attend_back_head(
            qkv_ref, ctx_ref, inv_ref, back_ref, segc_ref, segr_ref, grad_ref.at[0], bias_ref, key_acc, value_acc, 0, head, cols, tile
        )


def attend_back(residual_half, weights, qkv, context, inverse, segments, cols, tile):
    rows, width = residual_half.shape
    slots, _, lanes = weights.shape
    heads = cols // DH
    whole = lambda shape: pl.BlockSpec(shape, lambda s: (0,) * len(shape))
    each = lambda shape: pl.BlockSpec((1,) + shape, lambda s: (s, 0, 0))
    return pl.pallas_call(
        functools.partial(attend_back_kernel, cols=cols, tile=tile),
        grid=(slots,),
        in_specs=[
            whole((rows, width)),
            each((width, lanes)),
            each((rows, 3 * cols)),
            each((rows, cols)),
            each((rows, heads)),
            whole((rows, 1)),
            whole((rows // tile, 1, tile)),
        ],
        out_specs=[each((rows, 3 * cols)), each((2, cols))],
        out_shape=[
            jax.ShapeDtypeStruct((slots, rows, 3 * cols), BF16),
            jax.ShapeDtypeStruct((slots, 2, cols), F32),
        ],
        scratch_shapes=[
            pltpu.VMEM((rows, cols), BF16),
            pltpu.VMEM((rows, DH), F32),
            pltpu.VMEM((rows, DH), F32),
        ],
        cost_estimate=pl.CostEstimate(
            flops=slots * (2 * rows * width * cols + 10 * rows * rows * 256 * heads),
            bytes_accessed=slots * width * lanes * 2 + rows * width * 10,
            transcendentals=slots * heads * rows * rows,
        ),
        name="attend_back",
    )(residual_half, weights, qkv, context, inverse, segments[:, None], segments.reshape(-1, 1, tile))


def plain_layer(shards, vectors, to_slot, from_slot, block_input, cotangent, gains, shifts, segments, owned, cols, units, parts):
    width, rows = block_input.shape[2], segments.shape[0]
    slots, slot = lax.axis_size("slot"), lax.axis_index("slot")
    main_units, in_lanes = shards[1].shape[1], 3 * cols
    rest = units - main_units
    spare = shards[0].shape[1] - in_lanes - cols - 2 * rest
    small_all, up_main, down_main = gather_weights(shards)
    vec_all = lax.all_gather(vectors, "slot", axis=0)
    grad_rows = jnp.where(owned[:, None], to_slot(cotangent), 0)
    upstream = grad_rows.astype(F32)
    x_float = to_slot(block_input).astype(F32)
    first_out, first_scaled, first_factor = norm_forward(x_float, gains[0], shifts[0])
    first_norm = first_out.astype(BF16)
    bias = vec_all[:, :1, :in_lanes].astype(F32) + vec_all[:, 1:2, :in_lanes].astype(F32)
    qkv, context, inverse, attention_part = attend(first_norm, small_all, bias, segments, cols, rows // 2)
    residual = x_float + part_sum(attention_part, parts) + shifts[2]
    second_out, second_scaled, second_factor = norm_forward(residual, gains[1], shifts[1])
    second_norm = second_out.astype(BF16)
    small_blocks = list(small_all)
    unit_all = vec_all[:, 2, :units].astype(F32)
    at = in_lanes + cols
    ups = list(up_main) + [b[:, at : at + rest] for b in small_blocks]
    downs = list(down_main) + [b[:, at + rest : at + 2 * rest] for b in small_blocks]
    unit_rows = list(unit_all[:, :main_units]) + list(unit_all[:, main_units:])
    pre_acts = [dot_nn(second_norm, w) + b for w, b in zip(ups, unit_rows)]
    hiddens = [gelu(p).astype(BF16) for p in pre_acts]
    output = (residual + part_sum(sum_products(hiddens, downs), parts) + shifts[3]).astype(BF16)
    down_sums = [dot_tn(grad_rows, h).astype(BF16) for h in hiddens]
    pre_grads = [gelu_back(p, dot_nn(grad_rows, w)) for p, w in zip(pre_acts, downs)]
    pre_halves = [p.astype(BF16) for p in pre_grads]
    unit_sums = [jnp.sum(p, axis=0) for p in pre_grads]
    up_sums = [dot_tn(second_norm, p).astype(BF16) for p in pre_halves]
    second_grad = part_sum(sum_products(pre_halves, ups), parts)
    residual_grad = upstream + norm_backward(second_grad, second_scaled, second_factor, gains[1])
    residual_half = residual_grad.astype(BF16)
    triple, bias_sum = attend_back(residual_half, small_all, qkv, context, inverse, segments, cols, rows // 2)
    first_part = sum_products(list(triple), [b[:, :in_lanes] for b in small_blocks])
    first_grad = part_sum(first_part, parts)
    input_grad = residual_grad + norm_backward(first_grad, first_scaled, first_factor, gains[0])
    blank = jnp.zeros((width, spare), BF16)
    small_sums = [
        jnp.concatenate(
            [
                dot_tn(first_norm, triple[s]).astype(BF16),
                dot_tn(residual_half, context[s]).astype(BF16),
                up_sums[slots + s],
                down_sums[slots + s],
                blank,
            ],
            axis=1,
        )
        for s in range(slots)
    ]
    down_grad, up_grad, small_grad = scatter_grads(
        [jnp.stack(down_sums[:slots]), jnp.stack(up_sums[:slots]), jnp.stack(small_sums)]
    )
    rows_sum = jnp.stack(
        [
            jnp.sum(first_grad * first_scaled, axis=0),
            jnp.sum(second_grad * second_scaled, axis=0),
            jnp.sum(first_grad, axis=0),
            jnp.sum(second_grad, axis=0),
            jnp.sum(residual_grad, axis=0),
            jnp.sum(upstream, axis=0),
        ]
    )
    unit_sum = jnp.stack([jnp.concatenate([unit_sums[s], unit_sums[slots + s]]) for s in range(slots)])
    rows_total, bias_total, unit_total = lax.psum((rows_sum, bias_sum, unit_sum), ("slot",) + FSDP)
    bias_grad = lax.dynamic_index_in_dim(bias_total, slot, 0, keepdims=False)
    unit_grad = lax.dynamic_index_in_dim(unit_total, slot, 0, keepdims=False)
    return (
        from_slot(output, owned), from_slot(input_grad.astype(BF16), owned), rows_total, bias_grad, unit_grad,
        down_grad, up_grad, small_grad,
    )


def on_device(
    block_input,
    segment_ids,
    norm_gains,
    row_biases,
    in_projection,
    query_value_bias,
    out_projection,
    up_weight,
    unit_bias,
    down_weight,
    cotangent,
):
    local, rows_each, width = block_input.shape
    rows_mb = segment_ids.shape[1]
    cols = in_projection.shape[2]
    units = up_weight.shape[1]
    shard_rows = up_weight.shape[0]
    slots, parts = lax.axis_size("slot"), lax.axis_size("part")
    slot, part = lax.axis_index("slot"), lax.axis_index("part")
    fsdp_index = lax.axis_index("fy") * lax.axis_size("fx") + lax.axis_index("fx")
    batch, image = slot % local, slot // local
    late = image == 1

    half_rows = rows_mb // IMG_MB
    padding = rows_mb - IMG_MB * IMG
    edge = round_up(max(half_rows - IMG, padding - (half_rows - IMG)), 16)
    tail = round_up(padding, 16)
    rows = round_up(half_rows + edge + tail, 128)
    filler = rows - half_rows - edge - tail
    paired = lax.axis_size("fy") == 2 and lax.axis_size("fx") == 2 and slots == 4 and parts == 2
    paired = paired and shard_rows % 32 == 0 and filler == 0

    def edges(main):
        near = jnp.where(late, main[:edge], main[half_rows - edge :])
        far = main[half_rows - tail :]
        return jnp.concatenate([near, far])

    def to_slot(value):
        mine = lax.dynamic_index_in_dim(value, batch, 0, keepdims=False)
        send = lax.dynamic_index_in_dim(value, 1 - batch, 0, keepdims=False)
        other = slot_swap(send, 1, slots)
        pair = jnp.where(batch == 0, jnp.stack([mine, other]), jnp.stack([other, mine]))
        main = part_gather(pair, parts).swapaxes(0, 1).reshape(half_rows, width)
        beyond = slot_swap(edges(main), local, slots)
        return jnp.concatenate([main, beyond, jnp.zeros((filler, width), value.dtype)])

    def from_slot(value, owned):
        main = value[:half_rows]
        beyond = slot_swap(value[half_rows : half_rows + edge + tail], local, slots)
        keep = owned[:half_rows, None]
        near, far = beyond[:edge], beyond[edge:]
        blank = lambda count: jnp.zeros((count, width), value.dtype)
        early_fill = jnp.concatenate([blank(half_rows - edge), near])
        late_fill = jnp.concatenate([near, blank(half_rows - edge - tail), far])
        main = jnp.where(keep, main, jnp.where(late, late_fill, early_fill))
        main = main.reshape(local, parts, rows_each, width)
        mine = lax.dynamic_index_in_dim(main, part, 1, keepdims=False)
        stay = lax.dynamic_index_in_dim(mine, batch, 0, keepdims=False)
        other = slot_swap(lax.dynamic_index_in_dim(mine, 1 - batch, 0, keepdims=False), 1, slots)
        return jnp.where(batch == 0, jnp.stack([stay, other]), jnp.stack([other, stay]))

    ids = jnp.where(batch == 0, segment_ids[:1], segment_ids[1:])
    filler_ids = lambda count: jnp.full((1, count), -2, jnp.int32)
    early_ids = jnp.concatenate([ids[:, : half_rows + edge], ids[:, rows_mb - tail :], filler_ids(filler)], axis=1)
    late_ids = jnp.concatenate(
        [ids[:, half_rows:], ids[:, half_rows - edge : half_rows], filler_ids(tail + filler)], axis=1
    )
    segr = jnp.where(late, late_ids, early_ids)
    segc = segr.reshape(rows, 1)

    main_units = units // 128 * 128
    rest = units - main_units
    in_lanes = 3 * cols
    small = in_lanes + cols + 2 * rest
    lanes = round_up(small, 128)
    gains, shifts = norm_gains, row_biases
    if paired:
        (
            small_all, up_main, down_main, gd, x_half, cot, first_norm, qkv, context, inverse, residual, second_norm,
            hidden, slope, hidden_rest, slope_rest, rest_up, rest_down,
        ) = forward_stage(
            (in_projection, out_projection, up_weight, down_weight), (query_value_bias, unit_bias.reshape(1, units)),
            block_input, cotangent, gains, shifts, segc, segr, cols, units, lanes, edge, tail,
        )
        gu, down_sum, rest_sums, residual_half, residual_grad, y_rows, sums, unit_sums, unit_rest_sums = middle_stage(
            down_main, up_main, gd, hidden, slope, hidden_rest, slope_rest, rest_up, rest_down, cot, second_norm, residual,
            gains, shifts, cols, rest, lanes - small,
        )
        in_grad, out_grad, up_grad, down_grad, input_grad, output, gain_grad, shift_grad, bias_grad, unit_grad = backward_stage(
            small_all, gu, rest_sums, residual_half, first_norm, qkv, context, inverse, segc, segr, x_half, residual_grad,
            y_rows, gains, down_sum, sums, unit_sums, unit_rest_sums, cols, rest, edge, tail, rows_each,
        )
        unit_grad = unit_grad.reshape(units)
    else:
        segments = segc[:, 0]
        image_id = (fsdp_index * local + batch) * IMG_MB + image
        owned = (segments == image_id) | (jnp.logical_not(late) & (segments == -1))
        down_t = down_weight.T
        small_shard = jnp.concatenate(
            [
                in_projection.transpose(1, 0, 2).reshape(shard_rows, in_lanes),
                out_projection.T,
                up_weight[:, main_units:],
                down_t[:, main_units:],
                jnp.zeros((shard_rows, lanes - small), BF16),
            ],
            axis=1,
        )
        shards = [small_shard, up_weight[:, :main_units], down_t[:, :main_units]]
        triple_bias = jnp.concatenate([query_value_bias[0], jnp.zeros((cols,), F32), query_value_bias[1]])
        high = triple_bias.astype(BF16)
        low = (triple_bias - high.astype(F32)).astype(BF16)
        wide = round_up(max(in_lanes, units), 128)
        vectors = [jnp.pad(v, (0, wide - v.shape[0])) for v in (high, low, unit_bias)]
        vectors = jnp.concatenate([jnp.stack(vectors), jnp.zeros((13, wide), BF16)])
        output, input_grad, rows_total, bias_grad, unit_grad, down_grad, up_grad, small_grad = plain_layer(
            shards, vectors, to_slot, from_slot, block_input, cotangent, gains, shifts, segments, owned, cols, units, parts
        )
        in_grad = small_grad[:, :in_lanes].reshape(shard_rows, 3, cols).transpose(1, 0, 2)
        out_grad = small_grad[:, in_lanes : in_lanes + cols].T
        at = in_lanes + cols
        up_grad = jnp.concatenate([up_grad, small_grad[:, at : at + rest]], axis=1)
        down_grad = jnp.concatenate([down_grad, small_grad[:, at + rest : at + 2 * rest]], axis=1).T
        gain_grad, shift_grad = rows_total[:2], rows_total[2:]
    return (
        output,
        input_grad.astype(F32),
        gain_grad,
        shift_grad,
        in_grad,
        bias_grad,
        out_grad,
        up_grad,
        unit_grad,
        down_grad,
    )


def solution(mesh):
    fsdp, tensor = mesh.shape["fsdp"], mesh.shape["tensor"]

    def layer(*arrays):
        local = arrays[0].shape[0] // fsdp
        slots = local * IMG_MB
        assert local == 2 and slots == 4 and tensor % slots == 0 and fsdp % 2 == 0
        grid = Mesh(
            mesh.devices.reshape(fsdp // 2, 2, slots, tensor // slots), ("fy", "fx", "slot", "part")
        )
        tens = ("slot", "part")
        return jax.shard_map(
            on_device,
            mesh=grid,
            in_specs=(
                P(FSDP, tens, None),
                P(FSDP, None),
                P(),
                P(),
                P(None, FSDP, tens),
                P(None, tens),
                P(tens, FSDP),
                P(FSDP, tens),
                P(tens),
                P(tens, FSDP),
                P(FSDP, tens, None),
            ),
            out_specs=(
                P(FSDP, tens, None),
                P(FSDP, tens, None),
                P(),
                P(),
                P(None, FSDP, tens),
                P(None, tens),
                P(tens, FSDP),
                P(FSDP, tens),
                P(tens),
                P(tens, FSDP),
            ),
            check_vma=False,
        )(*arrays)

    return layer
```

profile of v0, /device:TPU:0, one launch (start us, length us, event | category | flops | bytes accessed | tf_op | source)
XLA Modules:
  0.0 356.5 jit_solution(4202476318848324111)
XLA Ops:
  0.7 1.3 reshape.153.refs_5_
  1.9 0.1 pad.9.clone
  2.0 0.8 broadcast_select_fusion.1
  2.8 0.1 fusion.1
  2.9 0.1 fusion.3
  3.0 0.7 broadcast_select_fusion.2.refs_11_.refs_9_
  3.6 0.1 pad_add_fusion
  3.7 1.9 copy.38.refs_3_
  5.6 1.9 copy.37.refs_0_
  7.6 0.2 copy.36
  7.8 0.2 copy.35
  8.0 0.8 broadcast_select_fusion.refs_10_.refs_8_
  8.8 147.1 %forward.1 = (bf16[4,1152,640]{2,1,0:T(8,128)(2,1)}, bf16[4,1152,512]{2,1,0:T(8,128)(2,1)}, bf16[4,1152,512]{2,1,0:T(8,128)(2,1)}, bf16[4,1152,512]{2,1,0:T(8,12...) custom-call(bf16[3,288,144]{2,1,0:T(8,128)(2,1)} %copy.37.refs_0_, ...), custom_call_target="tpu_custom_call" | custom-call | tf_op jit(solution)/shard_map/forward/pallas_call | solution.py:654
  155.9 72.6 %middle.1 = (bf16[4,1152,512]{2,1,0:T(8,128)(2,1)}, f32[512,288]{1,0:T(8,128)}, bf16[4,1152,64]{2,1,0:T(8,128)(2,1)}, bf16[896,1152]{1,0:T(8,128)(2,1)}, f32[896...) custom-call(bf16[4,1152,512]{2,1,0:T(8,128)(2,1)} %get-tuple-element, ...), custom_call_target="tpu_custom_call" | custom-call | tf_op jit(solution)/shard_map/middle/pallas_call | solution.py:864
  228.5 116.3 %backward.1 = (f32[3,288,144]{2,1,0:T(8,128)}, f32[144,288]{1,0:T(8,128)}, f32[288,538]{1,0:T(8,128)}, f32[538,288]{1,0:T(8,128)}, f32[2,192,1152]{2,1,0:T(8,128...) custom-call(bf16[4,1152,640]{2,1,0:T(8,128)(2,1)} %get-tuple-element, ...), custom_call_target="tpu_custom_call" | custom-call | tf_op jit(solution)/shard_map/backward/pallas_call | solution.py:1367
  344.8 0.0 copy-start.1
  344.8 1.4 reduce
  346.2 0.0 copy-start
  346.2 2.5 copy.39
  348.7 2.3 copy.40
  351.0 0.0 copy-done.1
  351.0 0.9 copy.48
  351.9 0.0 copy-done
  351.9 0.0 copy-start.5
  351.9 0.0 copy-start.4
  351.9 0.0 copy-start.6
  351.9 0.0 copy-start.3
  351.9 0.0 copy-start.2
  351.9 1.2 copy.49
  353.1 0.0 copy-done.5
  353.1 0.6 copy.50
  353.7 0.0 copy-done.4
  353.7 0.6 copy.51
  354.4 0.0 copy-done.6
  354.4 0.6 copy.52
  354.9 0.0 copy-done.3
  354.9 0.7 copy.53
  355.6 0.0 copy-done.2
  355.6 0.9 copy.54
  (4 shorter events, 0.0 us)
Async XLA Ops:
  344.8 6.2 %copy-start.1 = (bf16[2,192,1152]{2,1,0:T(8,128)(2,1)S(1)}, bf16[2,192,1152]{2,1,0:T(8,128)(2,1)}, u32[]{:S(2)}) copy-start(bf16[2,192,1152]{2,1,0:T(8,128)(2,1)} %get-tuple-element.132) | copy-start | bytes 2654212
  346.2 5.7 %copy-start = (f32[2,192,1152]{2,1,0:T(8,128)S(1)}, f32[2,192,1152]{2,1,0:T(8,128)}, u32[]{:S(2)}) copy-start(f32[2,192,1152]{2,1,0:T(8,128)} %get-tuple-element.133) | copy-start | bytes 5308420
  351.9 1.2 copy-start.5
  351.9 1.8 copy-start.4
  351.9 2.4 copy-start.6
  351.9 3.0 copy-start.3
  351.9 3.7 %copy-start.2 = (f32[288,538]{1,0:T(8,128)S(1)}, f32[288,538]{1,0:T(8,128)}, u32[]{:S(2)}) copy-start(f32[288,538]{1,0:T(8,128)} %get-tuple-element.139) | copy-start | bytes 1859332
where the time goes:
time: 357 us; the launch traced here: 356 us
  Pallas kernels  336 us (94%)
  local copies, waits for them, and re-layouts  16.1 us (5%)
  other arithmetic  3.71 us (1%)
    pallas_call x1, Pallas kernels, forward_stage(): pl.pallas_call(functools.partial(forward_kernel, cols=cols, unit_rest=uni...  147 us
    pallas_call x1, Pallas kernels, backward_stage(): pl.pallas_call(functools.partial(backward_kernel, cols=cols, unit_rest=un...  116 us
    pallas_call x1, Pallas kernels, middle_stage(): pl.pallas_call(functools.partial(middle_kernel, cols=cols, unit_rest=unit...  72.6 us
    unnamed x25, local copies, waits for them, and re-layouts  14.1 us

commit v1 on v0

--- a/solution.py
+++ b/solution.py
@@ -127,6 +127,9 @@
     def owned(self, segments):
         mine = segments == (self.f * 2 + self.batch) * IMG_MB + self.image
         return mine | ((segments == -1) & (self.image == 0))
+
+    def behind(self):
+        return jnp.where((self.z == 1) | (self.z == 2), 1, 0)
 
     def slot_after(self, d):
         return {"slot": (self.z + d) % 4}
@@ -419,12 +422,12 @@
     rows, width = x_ref.shape
     place = Place()
     for n in range(3):
-        small_ref[:, n * cols : (n + 1) * cols] = in_ref[n]
+        small_ref[:, n * cols : (n + 1) * cols] = in_ref[n].T
     at = 3 * cols
     small_ref[:, at : at + cols] = out_ref[...].T
     at = at + cols
     small_ref[:, at : at + rest] = up_whole[:, main:]
-    small_ref[:, at + rest : at + 2 * rest] = down_whole[main:, :].T
+    small_ref[:, at + rest : at + 2 * rest] = down_whole[:, main:]
     at = at + 2 * rest
     if at < small_ref.shape[1]:
         small_ref[:, at:] = jnp.zeros((small_ref.shape[0], small_ref.shape[1] - at), BF16)
@@ -457,7 +460,7 @@
     x_rows.start()
     vec_all[place.z] = vec_ref[...]
     up_ref[...] = up_whole[:, :main]
-    down_ref[...] = down_whole[:main, :].T
+    down_ref[...] = down_whole[:, :main]
     g.pass_on(0, 1)
     g.corner(0, 0)
     x_rows.forward()
@@ -730,9 +733,9 @@
     place.barrier()
 
     def down_final(total):
-        d_out[...] = total[...].astype(F32).T
-
-    r = Reduce(place, (gd,), (d_own,), (down_final,), (d_bufs,), sems, loads, d_out.shape[1])
+        d_out[...] = total[...].astype(F32)
+
+    r = Reduce(place, (gd,), (d_own,), (down_final,), (d_bufs,), sems, loads, d_out.shape[0])
 
     def load(w, slot, buffer):
         return pltpu.make_async_copy(w.at[slot], blocks.at[buffer], load_sem.at[buffer])
@@ -790,44 +793,48 @@
     for h in (0, 1):
         part_out[halves(h), :] = part[halves(h), :].astype(BF16)
         exchange(0, h).start()
+    part[...] = dot_nt(half_rest, rest_up[...])
+
+    def up_block(s, carry):
+        load(wu, s, s % 2).wait()
+        pl.when(s < 3)(lambda: load(wu, s + 1, (s + 1) % 2).start())
+        part[...] += dot_nt(pre_half[s], blocks[s % 2])
+        return carry
+
+    lax.fori_loop(0, 4, up_block, 0)
     enter(1).wait()
     enter(2).wait()
+    for h in (0, 1):
+        exchange(0, h).wait_recv()
+
+    def output(span):
+        value = part_out[span, :].astype(F32) + part_in[span, :].astype(F32)
+        y_ref[span, :] = (res_ref[span, :] + value + shift_ref[3:4, :]).astype(BF16)
+
+    row_tiles(rows, 128, output)
+    for h in (0, 1):
+        exchange(0, h).wait_send()
+        part_out[halves(h), :] = part[halves(h), :].astype(BF16)
+        exchange(1, h).start()
+
+    def grad_out(s):
+        return pltpu.make_async_copy(grads.at[s % 2], gu.at[s], grad_sem.at[s % 2])
+
+    def up_grad(s, carry):
+        pl.when(s >= 2)(lambda: grad_out(s - 2).wait())
+        grads[s % 2] = dot_tn(second_ref[...], pre_half[s]).astype(BF16)
+        grad_out(s).start()
+        n = s - place.behind()
+        pl.when((n >= 0) & (n < 3))(lambda: r.line_one(0, n))
+        return carry
+
+    lax.fori_loop(0, 4, up_grad, 0)
     up_sum = dot_tn(second_ref[...], half_rest).astype(BF16)
     down_sum = dot_tn(c_ref[...], hidden_rest[...]).astype(BF16)
     rest_sums[...] = jnp.zeros_like(rest_sums)
     for s in range(4):
         rest_sums[s, :, :rest] = up_sum[:, s * rest : (s + 1) * rest]
         rest_sums[s, :, rest : 2 * rest] = down_sum[:, s * rest : (s + 1) * rest]
-    part[...] = dot_nt(half_rest, rest_up[...])
-
-    def grad_out(s):
-        return pltpu.make_async_copy(grads.at[s % 2], gu.at[s], grad_sem.at[s % 2])
-
-    def up_block(s, carry):
-        load(wu, s, s % 2).wait()
-        pl.when(s < 3)(lambda: load(wu, s + 1, (s + 1) % 2).start())
-        part[...] += dot_nt(pre_half[s], blocks[s % 2])
-        pl.when(s >= 2)(lambda: grad_out(s - 2).wait())
-        grads[s % 2] = dot_tn(second_ref[...], pre_half[s]).astype(BF16)
-        grad_out(s).start()
-        pl.when(s >= 2)(lambda: r.line_one(0, s - 2))
-        return carry
-
-    lax.fori_loop(0, 4, up_block, 0)
-    for h in (0, 1):
-        exchange(0, h).wait_recv()
-
-    def output(span):
-        value = part_out[span, :].astype(F32) + part_in[span, :].astype(F32)
-        y_ref[span, :] = (res_ref[span, :] + value + shift_ref[3:4, :]).astype(BF16)
-
-    row_tiles(rows, 128, output)
-    for h in (0, 1):
-        exchange(0, h).wait_send()
-        part_out[halves(h), :] = part[halves(h), :].astype(BF16)
-        exchange(1, h).start()
-    r.line_one(0, 2)
-    r.line_one(0, 3)
     for h in (0, 1):
         exchange(1, h).wait_recv()
     sums_ref[...] = jnp.zeros_like(sums_ref)
@@ -845,6 +852,7 @@
         sums_ref[5:6, :] += jnp.sum(upstream, axis=0, keepdims=True)
 
     row_tiles(rows, 128, back)
+    r.line_one(0, 3)
     for s in (2, 3):
         grad_out(s).wait()
     r.drain(0)
@@ -867,7 +875,7 @@
         out_specs=[far] + [vmem] * 8,
         out_shape=[
             shape((4, width, main), BF16),
-            shape((main, shard_rows), F32),
+            shape((shard_rows, main), F32),
             shape((4, width, 2 * unit_rest + spare), BF16),
             shape((rows, width), BF16),
             shape((rows, width), F32),
@@ -1181,12 +1189,12 @@
 
     def small_final(total):
         for n in range(3):
-            in_out[n] = total[:, n * cols : (n + 1) * cols].astype(F32)
+            in_out[n] = total[:, n * cols : (n + 1) * cols].astype(F32).T
         at = 3 * cols
         out_out[...] = total[:, at : at + cols].astype(F32).T
         at = at + cols
         up_out[:, main:] = total[:, at : at + rest].astype(F32)
-        down_out[main:, :] = total[:, at + rest : at + 2 * rest].astype(F32).T
+        down_out[:, main:] = total[:, at + rest : at + 2 * rest].astype(F32)
 
     r = Reduce(place, (gu, gs), (u_own, None), (up_final, small_final), (u_bufs, s_bufs), sems, loads, shard_rows)
     x_back = RowsBack(place, 0, part_in, inbox_x, segc_ref, x_out, back_sems, each, edge, tail)
@@ -1210,7 +1218,7 @@
     r.start(0)
     for t in range(rows // tile):
         segr_ref[t] = segr_whole[:, t * tile : (t + 1) * tile]
-    down_out[:main, :] = d_in[...]
+    down_out[:, :main] = d_in[...]
     first_load.start()
     for i in (1, 2, 3):
         for copy in slot_loads(i):
@@ -1253,7 +1261,7 @@
             part[...] += product
 
         r.start_one(1, s)
-        pl.when(i > 0)(lambda: r.line_one(0, i - 1))
+        pl.when(i > place.behind())(lambda: r.line_one(0, i - 1 - place.behind()))
         pl.when(i > 0)(lambda: r.middle_one(1, i - 1))
         return carry
 
@@ -1272,6 +1280,7 @@
         exchange(h).start()
     res_load = pltpu.make_async_copy(res_grad_ref, part, load_sem.at[0])
     res_load.start()
+    pl.when(place.behind() == 1)(lambda: r.line_one(0, 2))
     r.line_one(0, 3)
     pl.when((place.z == 0) | (place.z == 3))(lambda: r.line_one(1, 0))
     for h in (0, 1):
@@ -1369,10 +1378,10 @@
         in_specs=[far] * 2 + [vmem] * 2 + [far] * 4 + [vmem] * 2 + [far] * 3 + [vmem] * 5,
         out_specs=[vmem] * 10,
         out_shape=[
-            shape((3, shard_rows, cols), F32),
+            shape((3, cols, shard_rows), F32),
             shape((cols, shard_rows), F32),
             shape((shard_rows, main + unit_rest), F32),
-            shape((main + unit_rest, shard_rows), F32),
+            shape((shard_rows, main + unit_rest), F32),
             shape((2, rows_each, width), F32),
             shape((2, rows_each, width), BF16),
             shape((2, width), F32),
@@ -1731,7 +1740,7 @@
             small_all, up_main, down_main, gd, x_half, cot, first_norm, qkv, context, inverse, residual, second_norm,
             hidden, slope, hidden_rest, slope_rest, rest_up, rest_down,
         ) = forward_stage(
-            (in_projection, out_projection, up_weight, down_weight), (query_value_bias, unit_bias.reshape(1, units)),
+            (in_projection.swapaxes(1, 2), out_projection, up_weight, down_weight.T), (query_value_bias, unit_bias.reshape(1, units)),
             block_input, cotangent, gains, shifts, segc, segr, cols, units, lanes, edge, tail,
         )
         gu, down_sum, rest_sums, residual_half, residual_grad, y_rows, sums, unit_sums, unit_rest_sums = middle_stage(
@@ -1743,6 +1752,7 @@
             y_rows, gains, down_sum, sums, unit_sums, unit_rest_sums, cols, rest, edge, tail, rows_each,
         )
         unit_grad = unit_grad.reshape(units)
+        in_grad, down_grad = in_grad.swapaxes(1, 2), down_grad.T
     else:
         segments = segc[:, 0]
         image_id = (fsdp_index * local + batch) * IMG_MB + image

time: 357 us -> 345 us (0.966)
  Pallas kernels: 336 us -> 330 us
  local copies, waits for them, and re-layouts: 16.1 us -> 10.3 us
    unnamed x25, local copies, waits for them, and re-layouts: 14.1 us -> 8.42 us
    pallas_call x1, Pallas kernels: 72.6 us -> 67.4 us  [middle_stage(): pl.pallas_call(functools.partial(middle_kernel, cols=cols, unit_rest=unit...]
where the time goes in v1:
time: 345 us
  Pallas kernels  330 us (96%)
  local copies, waits for them, and re-layouts  10.3 us (3%)
  other arithmetic  3.75 us (1%)
    pallas_call x1, Pallas kernels, forward_stage(): pl.pallas_call(functools.partial(forward_kernel, cols=cols, unit_rest=uni...  147 us
    pallas_call x1, Pallas kernels, backward_stage(): pl.pallas_call(functools.partial(backward_kernel, cols=cols, unit_rest=un...  116 us
    pallas_call x1, Pallas kernels, middle_stage(): pl.pallas_call(functools.partial(middle_kernel, cols=cols, unit_rest=unit...  67.4 us
    unnamed x25, local copies, waits for them, and re-layouts  8.42 us

profile of v1, /device:TPU:0, one launch (start us, length us, event | category | flops | bytes accessed | tf_op | source)
XLA Modules:
  0.0 345.1 jit_solution(7550871192070645882)
XLA Ops:
  0.7 1.3 reshape.153.refs_5_
  1.9 0.1 pad.9.clone
  2.0 0.8 broadcast_select_fusion.1
  2.8 0.1 fusion.1
  2.9 0.1 fusion.3
  3.0 0.7 broadcast_select_fusion.2.refs_11_.refs_9_
  3.6 0.1 pad_add_fusion
  3.7 0.2 copy.28
  3.9 0.2 copy.27
  4.1 0.8 broadcast_select_fusion.refs_10_.refs_8_
  5.0 147.1 %forward.1 = (bf16[4,1152,640]{2,1,0:T(8,128)(2,1)}, bf16[4,1152,512]{2,1,0:T(8,128)(2,1)}, bf16[4,1152,512]{2,1,0:T(8,128)(2,1)}, bf16[4,1152,512]{2,1,0:T(8,12...) custom-call(bf16[3,144,288]{2,1,0:T(8,128)(2,1)} %bitcast.15, ...), custom_call_target="tpu_custom_call" | custom-call | tf_op jit(solution)/shard_map/forward/pallas_call | solution.py:657
  152.1 67.4 %middle.1 = (bf16[4,1152,512]{2,1,0:T(8,128)(2,1)}, f32[288,512]{1,0:T(8,128)}, bf16[4,1152,64]{2,1,0:T(8,128)(2,1)}, bf16[896,1152]{1,0:T(8,128)(2,1)}, f32[896...) custom-call(bf16[4,1152,512]{2,1,0:T(8,128)(2,1)} %get-tuple-element, ...), custom_call_target="tpu_custom_call" | custom-call | tf_op jit(solution)/shard_map/middle/pallas_call | solution.py:872
  219.5 115.8 %backward.1 = (f32[3,144,288]{2,1,0:T(8,128)}, f32[144,288]{1,0:T(8,128)}, f32[288,538]{1,0:T(8,128)}, f32[288,538]{1,0:T(8,128)}, f32[2,192,1152]{2,1,0:T(8,128...) custom-call(bf16[4,1152,640]{2,1,0:T(8,128)(2,1)} %get-tuple-element, ...), custom_call_target="tpu_custom_call" | custom-call | tf_op jit(solution)/shard_map/backward/pallas_call | solution.py:1376
  335.2 0.0 copy-start
  335.3 1.4 reduce
  336.6 2.1 copy.38
  338.8 0.0 copy-done
  338.8 0.0 copy-start.6
  338.8 0.0 copy-start.5
  338.8 0.0 copy-start.3
  338.8 0.0 copy-start.7
  338.8 0.0 copy-start.4
  338.8 0.0 copy-start.2
  338.8 1.2 copy.39
  340.0 0.0 copy-done.6
  340.0 0.0 copy-start.1
  340.1 0.6 copy.40
  340.6 0.0 copy-done.5
  340.7 0.6 copy.41
  341.3 0.0 copy-done.3
  341.3 0.8 copy.42
  342.1 0.0 copy-done.7
  342.1 0.6 copy.43
  342.7 0.0 copy-done.4
  342.7 0.7 copy.44
  343.4 0.0 copy-done.2
  343.4 0.9 copy.45
  344.2 0.0 copy-done.1
  344.2 0.9 copy.46
  (4 shorter events, 0.0 us)
Async XLA Ops:
  335.2 3.6 %copy-start = (f32[2,192,1152]{2,1,0:T(8,128)S(1)}, f32[2,192,1152]{2,1,0:T(8,128)}, u32[]{:S(2)}) copy-start(f32[2,192,1152]{2,1,0:T(8,128)} %get-tuple-element.103) | copy-start | bytes 5308420
  338.8 1.3 copy-start.6
  338.8 1.9 copy-start.5
  338.8 2.5 copy-start.3
  338.8 3.3 copy-start.7
  338.8 3.9 %copy-start.4 = (f32[144,288]{1,0:T(8,128)S(1)}, f32[144,288]{1,0:T(8,128)}, u32[]{:S(2)}) copy-start(f32[144,288]{1,0:T(8,128)} %get-tuple-element.108) | copy-start | bytes 497668
  338.8 4.5 %copy-start.2 = (f32[288,538]{1,0:T(8,128)S(1)}, f32[288,538]{1,0:T(8,128)}, u32[]{:S(2)}) copy-start(f32[288,538]{1,0:T(8,128)} %get-tuple-element.109) | copy-start | bytes 1859332
  340.0 4.2 %copy-start.1 = (f32[288,538]{1,0:T(8,128)S(1)}, f32[288,538]{1,0:T(8,128)}, u32[]{:S(2)}) copy-start(f32[288,538]{1,0:T(8,128)} %get-tuple-element.83) | copy-start | bytes 1859332

commit v2 on v1

--- a/solution.py
+++ b/solution.py
@@ -1263,6 +1263,7 @@
         r.start_one(1, s)
         pl.when(i > place.behind())(lambda: r.line_one(0, i - 1 - place.behind()))
         pl.when(i > 0)(lambda: r.middle_one(1, i - 1))
+        pl.when(i > 1 + place.behind())(lambda: r.line_one(1, i - 2 - place.behind()))
         return carry
 
     lax.fori_loop(0, 4, one_slot, 0)
@@ -1282,7 +1283,8 @@
     res_load.start()
     pl.when(place.behind() == 1)(lambda: r.line_one(0, 2))
     r.line_one(0, 3)
-    pl.when((place.z == 0) | (place.z == 3))(lambda: r.line_one(1, 0))
+    pl.when(place.behind() == 1)(lambda: r.line_one(1, 1))
+    r.middle_one(1, 3)
     for h in (0, 1):
         exchange(h).wait_recv()
 
@@ -1331,14 +1333,11 @@
 
     for copy in across(0, place.across_x):
         copy.start()
-    r.middle_one(1, 3)
-    pl.when((place.z == 1) | (place.z == 2))(lambda: r.line_one(1, 0))
-    r.line_one(1, 1)
+    r.line_one(1, 2)
     add_across(0, place.across_x)
     for copy in across(1, place.across_y):
         copy.start()
     x_back.finish()
-    r.line_one(1, 2)
     add_across(1, place.across_y)
     for d in (1, 2, 3):
         for copy in along(d):

time: 345 us -> 343 us (level)
  no operation moved by 1% of the time
where the time goes in v2:
time: 343 us; the launch traced here: 342 us
  Pallas kernels  327 us (95%)
  local copies, waits for them, and re-layouts  10.3 us (3%)
  other arithmetic  3.75 us (1%)
    pallas_call x1, Pallas kernels, forward_stage(): pl.pallas_call(functools.partial(forward_kernel, cols=cols, unit_rest=uni...  147 us
    pallas_call x1, Pallas kernels, backward_stage(): pl.pallas_call(functools.partial(backward_kernel, cols=cols, unit_rest=un...  113 us
    pallas_call x1, Pallas kernels, middle_stage(): pl.pallas_call(functools.partial(middle_kernel, cols=cols, unit_rest=unit...  67.4 us
    unnamed x25, local copies, waits for them, and re-layouts  8.42 us

profile of v2, /device:TPU:0, one launch (start us, length us, event | category | flops | bytes accessed | tf_op | source)
XLA Modules:
  0.0 342.2 jit_solution(12521985449824113349)
XLA Ops:
  0.7 1.3 reshape.153.refs_5_
  1.9 0.1 pad.9.clone
  2.0 0.8 broadcast_select_fusion.1
  2.8 0.1 fusion.1
  2.9 0.1 fusion.3
  3.0 0.7 broadcast_select_fusion.2.refs_11_.refs_9_
  3.6 0.1 pad_add_fusion
  3.7 0.2 copy.28
  3.9 0.2 copy.27
  4.1 0.8 broadcast_select_fusion.refs_10_.refs_8_
  5.0 147.1 %forward.1 = (bf16[4,1152,640]{2,1,0:T(8,128)(2,1)}, bf16[4,1152,512]{2,1,0:T(8,128)(2,1)}, bf16[4,1152,512]{2,1,0:T(8,128)(2,1)}, bf16[4,1152,512]{2,1,0:T(8,12...) custom-call(bf16[3,144,288]{2,1,0:T(8,128)(2,1)} %bitcast.15, ...), custom_call_target="tpu_custom_call" | custom-call | tf_op jit(solution)/shard_map/forward/pallas_call | solution.py:657
  152.1 67.4 %middle.1 = (bf16[4,1152,512]{2,1,0:T(8,128)(2,1)}, f32[288,512]{1,0:T(8,128)}, bf16[4,1152,64]{2,1,0:T(8,128)(2,1)}, bf16[896,1152]{1,0:T(8,128)(2,1)}, f32[896...) custom-call(bf16[4,1152,512]{2,1,0:T(8,128)(2,1)} %get-tuple-element, ...), custom_call_target="tpu_custom_call" | custom-call | tf_op jit(solution)/shard_map/middle/pallas_call | solution.py:872
  219.5 112.8 %backward.1 = (f32[3,144,288]{2,1,0:T(8,128)}, f32[144,288]{1,0:T(8,128)}, f32[288,538]{1,0:T(8,128)}, f32[288,538]{1,0:T(8,128)}, f32[2,192,1152]{2,1,0:T(8,128...) custom-call(bf16[4,1152,640]{2,1,0:T(8,128)(2,1)} %get-tuple-element, ...), custom_call_target="tpu_custom_call" | custom-call | tf_op jit(solution)/shard_map/backward/pallas_call | solution.py:1375
  332.3 0.0 copy-start
  332.3 1.4 reduce
  333.7 2.1 copy.38
  335.9 0.0 copy-done
  335.9 0.0 copy-start.6
  335.9 0.0 copy-start.5
  335.9 0.0 copy-start.3
  335.9 0.0 copy-start.7
  335.9 0.0 copy-start.4
  335.9 0.0 copy-start.2
  335.9 1.2 copy.39
  337.1 0.0 copy-done.6
  337.1 0.0 copy-start.1
  337.1 0.6 copy.40
  337.7 0.0 copy-done.5
  337.7 0.6 copy.41
  338.3 0.0 copy-done.3
  338.3 0.8 copy.42
  339.2 0.0 copy-done.7
  339.2 0.6 copy.43
  339.8 0.0 copy-done.4
  339.8 0.7 copy.44
  340.4 0.0 copy-done.2
  340.4 0.9 copy.45
  341.3 0.0 copy-done.1
  341.3 0.9 copy.46
  (4 shorter events, 0.0 us)
Async XLA Ops:
  332.3 3.6 %copy-start = (f32[2,192,1152]{2,1,0:T(8,128)S(1)}, f32[2,192,1152]{2,1,0:T(8,128)}, u32[]{:S(2)}) copy-start(f32[2,192,1152]{2,1,0:T(8,128)} %get-tuple-element.103) | copy-start | bytes 5308420
  335.9 1.3 copy-start.6
  335.9 1.9 copy-start.5
  335.9 2.5 copy-start.3
  335.9 3.3 copy-start.7
  335.9 3.9 %copy-start.4 = (f32[144,288]{1,0:T(8,128)S(1)}, f32[144,288]{1,0:T(8,128)}, u32[]{:S(2)}) copy-start(f32[144,288]{1,0:T(8,128)} %get-tuple-element.108) | copy-start | bytes 497668
  335.9 4.5 %copy-start.2 = (f32[288,538]{1,0:T(8,128)S(1)}, f32[288,538]{1,0:T(8,128)}, u32[]{:S(2)}) copy-start(f32[288,538]{1,0:T(8,128)} %get-tuple-element.109) | copy-start | bytes 1859332
  337.1 4.2 %copy-start.1 = (f32[288,538]{1,0:T(8,128)S(1)}, f32[288,538]{1,0:T(8,128)}, u32[]{:S(2)}) copy-start(f32[288,538]{1,0:T(8,128)} %get-tuple-element.83) | copy-start | bytes 1859332

commit v3 on v2

--- a/solution.py
+++ b/solution.py
@@ -437,7 +437,7 @@
         lo = 2 * n * cols
         vec_ref[0:1, lo : lo + cols] = high
         vec_ref[1:2, lo : lo + cols] = (qv_ref[n : n + 1, :] - high.astype(F32)).astype(BF16)
-    vec_ref[2:3, : main + rest] = unit_ref[...]
+    vec_ref[2:3, : main + rest] = unit_ref[...].reshape(1, main + rest)
     place.barrier()
     shards = (small_ref, up_ref, down_ref)
     g = Gather(place, shards, (ws, wu, wd), gather_sems, local_sem, small_ref.shape[0])
@@ -1351,8 +1351,8 @@
     shift_out[...] = sums_ref[2:6, :]
     total = vec_sum[place.z] + vec_far[0] + vec_far[1] + vec_far[2]
     qv_out[...] = total[0:2, :cols]
-    unit_out[:, :main] = total[2:3, :main]
-    unit_out[:, main:] = total[3:4, :rest]
+    unit_out[:main] = total[2:3, :main].reshape(main)
+    unit_out[main:] = total[3:4, :rest].reshape(rest)
     for k in (0, 1):
         r.drain(k)
     x_back.drain()
@@ -1386,7 +1386,7 @@
             shape((2, width), F32),
             shape((4, width), F32),
             shape((2, cols), F32),
-            shape((1, main + unit_rest), F32),
+            shape((main + unit_rest,), F32),
         ],
         scratch_shapes=[
             pltpu.VMEM((2, 1, rows // 2), jnp.int32),
@@ -1739,7 +1739,7 @@
             small_all, up_main, down_main, gd, x_half, cot, first_norm, qkv, context, inverse, residual, second_norm,
             hidden, slope, hidden_rest, slope_rest, rest_up, rest_down,
         ) = forward_stage(
-            (in_projection.swapaxes(1, 2), out_projection, up_weight, down_weight.T), (query_value_bias, unit_bias.reshape(1, units)),
+            (in_projection.swapaxes(1, 2), out_projection, up_weight, down_weight.T), (query_value_bias, unit_bias),
             block_input, cotangent, gains, shifts, segc, segr, cols, units, lanes, edge, tail,
         )
         gu, down_sum, rest_sums, residual_half, residual_grad, y_rows, sums, unit_sums, unit_rest_sums = middle_stage(
@@ -1750,7 +1750,6 @@
             small_all, gu, rest_sums, residual_half, first_norm, qkv, context, inverse, segc, segr, x_half, residual_grad,
             y_rows, gains, down_sum, sums, unit_sums, unit_rest_sums, cols, rest, edge, tail, rows_each,
         )
-        unit_grad = unit_grad.reshape(units)
         in_grad, down_grad = in_grad.swapaxes(1, 2), down_grad.T
     else:
         segments = segc[:, 0]

time: 343 us -> 341 us (level)
    unnamed x25 -> x28, local copies, waits for them, and re-layouts: 8.42 us -> 9.15 us
where the time goes in v3:
time: 341 us; the launch traced here: 340 us
  Pallas kernels  327 us (96%)
  local copies, waits for them, and re-layouts  9.8 us (3%)
    pallas_call x1, Pallas kernels, forward_stage(): pl.pallas_call(functools.partial(forward_kernel, cols=cols, unit_rest=uni...  147 us
    pallas_call x1, Pallas kernels, backward_stage(): pl.pallas_call(functools.partial(backward_kernel, cols=cols, unit_rest=un...  113 us
    pallas_call x1, Pallas kernels, middle_stage(): pl.pallas_call(functools.partial(middle_kernel, cols=cols, unit_rest=unit...  67.4 us
    unnamed x28, local copies, waits for them, and re-layouts  9.15 us

profile of v3, /device:TPU:0, one launch (start us, length us, event | category | flops | bytes accessed | tf_op | source)
XLA Modules:
  0.0 340.3 jit_solution(6741220713881090061)
XLA Ops:
  0.7 0.1 pad.9.clone
  0.8 0.8 broadcast_select_fusion.1
  1.5 0.1 fusion.1
  1.6 0.1 fusion.3
  1.7 0.7 broadcast_select_fusion.2.refs_11_.refs_9_
  2.4 0.1 pad_add_fusion
  2.4 0.2 copy.28
  2.7 0.2 copy.27
  2.9 0.8 broadcast_select_fusion.refs_10_.refs_8_
  3.7 147.1 %forward.1 = (bf16[4,1152,640]{2,1,0:T(8,128)(2,1)}, bf16[4,1152,512]{2,1,0:T(8,128)(2,1)}, bf16[4,1152,512]{2,1,0:T(8,128)(2,1)}, bf16[4,1152,512]{2,1,0:T(8,12...) custom-call(bf16[3,144,288]{2,1,0:T(8,128)(2,1)} %bitcast.15, ...), custom_call_target="tpu_custom_call" | custom-call | tf_op jit(solution)/shard_map/forward/pallas_call | solution.py:657
  150.8 67.4 %middle.1 = (bf16[4,1152,512]{2,1,0:T(8,128)(2,1)}, f32[288,512]{1,0:T(8,128)}, bf16[4,1152,64]{2,1,0:T(8,128)(2,1)}, bf16[896,1152]{1,0:T(8,128)(2,1)}, f32[896...) custom-call(bf16[4,1152,512]{2,1,0:T(8,128)(2,1)} %get-tuple-element, ...), custom_call_target="tpu_custom_call" | custom-call | tf_op jit(solution)/shard_map/middle/pallas_call | solution.py:872
  218.2 112.9 %backward.1 = (f32[3,144,288]{2,1,0:T(8,128)}, f32[144,288]{1,0:T(8,128)}, f32[288,538]{1,0:T(8,128)}, f32[288,538]{1,0:T(8,128)}, f32[2,192,1152]{2,1,0:T(8,128...) custom-call(bf16[4,1152,640]{2,1,0:T(8,128)(2,1)} %get-tuple-element, ...), custom_call_target="tpu_custom_call" | custom-call | tf_op jit(solution)/shard_map/backward/pallas_call | solution.py:1375
  331.1 0.0 copy-start
  331.1 2.3 copy.39
  333.4 0.0 copy-done
  333.4 0.0 copy-start.6
  333.4 0.0 copy-start.5
  333.4 0.0 copy-start.3
  333.4 0.0 copy-start.8
  333.4 0.0 copy-start.4
  333.4 0.0 copy-start.2
  333.4 1.2 copy.40
  334.6 0.0 copy-done.6
  334.6 0.0 copy-start.7
  334.6 0.0 copy-start.1
  334.6 0.6 copy.41
  335.2 0.0 copy-done.5
  335.2 0.6 copy.42
  335.8 0.0 copy-done.3
  335.8 0.8 copy.43
  336.7 0.0 copy-done.8
  336.7 0.6 copy.44
  337.2 0.0 copy-done.4
  337.3 0.7 copy.45
  337.9 0.0 copy-done.2
  337.9 0.9 copy.46
  338.8 0.0 copy-done.7
  338.8 0.6 copy.47
  339.4 0.0 copy-done.1
  339.4 0.9 copy.48
  (4 shorter events, 0.0 us)
Async XLA Ops:
  331.1 2.3 copy-start
  333.4 1.3 copy-start.6
  333.4 1.9 copy-start.5
  333.4 2.5 copy-start.3
  333.4 3.3 copy-start.8
  333.4 3.9 %copy-start.4 = (f32[144,288]{1,0:T(8,128)S(1)}, f32[144,288]{1,0:T(8,128)}, u32[]{:S(2)}) copy-start(f32[144,288]{1,0:T(8,128)} %get-tuple-element.108) | copy-start | bytes 497668
  333.4 4.5 %copy-start.2 = (f32[288,538]{1,0:T(8,128)S(1)}, f32[288,538]{1,0:T(8,128)}, u32[]{:S(2)}) copy-start(f32[288,538]{1,0:T(8,128)} %get-tuple-element.109) | copy-start | bytes 1859332
  334.6 4.2 %copy-start.7 = (f32[538]{0:T(1024)S(1)}, f32[538]{0:T(1024)}, u32[]{:S(2)}) copy-start(f32[538]{0:T(1024)} %get-tuple-element.110) | copy-start | bytes 6460
  334.6 4.8 %copy-start.1 = (f32[288,538]{1,0:T(8,128)S(1)}, f32[288,538]{1,0:T(8,128)}, u32[]{:S(2)}) copy-start(f32[288,538]{1,0:T(8,128)} %get-tuple-element.83) | copy-start | bytes 1859332
